TPU v7x, 8 devices: a whole 2x2x1 slice. The times are simulated.
8 devices in a mesh: dp: 1 (over z), sp: 8 (over y, x, core).
Axes of the slice: x: 2, y: 2, z: 1, core: 2. Of those that a mesh axis runs over, the one named last changes fastest.
Arguments:
- hidden: bfloat16 [4096, 4096], P(('dp', 'sp'))
- positions: int32 [4096], P(('dp', 'sp'))
- d_attn: bfloat16 [4096, 4096], P(('dp', 'sp'))
- ln_weight: bfloat16 [4096], replicated
- w_q: bfloat16 [4096, 4096], replicated
- w_k: bfloat16 [4096, 1024], replicated
- w_v: bfloat16 [4096, 1024], replicated
- w_o: bfloat16 [4096, 4096], replicated
Outputs:
- output 1: bfloat16 [4096, 4096], P(('dp', 'sp'))
- output 2: bfloat16 [4096, 4096], P(('dp', 'sp'))
- output 3: bfloat16 [4096], P('dp')
- output 4: bfloat16 [4096, 4096], P('dp')
- output 5: bfloat16 [4096, 1024], P('dp')
- output 6: bfloat16 [4096, 1024], P('dp')
- output 7: bfloat16 [4096, 4096], P('dp')
All inputs are finite; a program needn't handle non-finite values.
Results may differ from a plain program's by a relative error of at most 0.0121239.
Values are sent between devices in bfloat16 or wider.
A program may use at most 1 GiB of HBM per device.

v0:
```python
import math
import jax
import jax.numpy as jnp
from jax import lax
from jax.sharding import PartitionSpec as P

HEAD_DIM = 128
LN_EPS = 1e-5
ROPE_BASE = 10000.0


def norm_f32(hid_f32, weight_f32):
    mean_val = jnp.mean(hid_f32, axis=-1, keepdims=True)
    centered = hid_f32 - mean_val
    var_val = jnp.mean(centered * centered, axis=-1, keepdims=True)
    return centered * lax.rsqrt(var_val + LN_EPS) * weight_f32


def rope_tables(positions):
    inv_freq = ROPE_BASE ** (-jnp.arange(0, HEAD_DIM, 2, dtype=jnp.float32) / HEAD_DIM)
    angles = positions.astype(jnp.float32)[:, None] * inv_freq[None, :]
    return jnp.cos(angles)[:, None, :], jnp.sin(angles)[:, None, :]


def apply_rope(values, cos_t, sin_t):
    rot_pairs = values.reshape(values.shape[:-1] + (HEAD_DIM // 2, 2))
    even_part = rot_pairs[..., 0]
    odd_part = rot_pairs[..., 1]
    new_even = even_part * cos_t - odd_part * sin_t
    new_odd = odd_part * cos_t + even_part * sin_t
    return jnp.stack([new_even, new_odd], axis=-1).reshape(values.shape)


def block_probs(q_block, row_start, k_all):
    scores = jnp.einsum('qgrd,kgd->grqk', q_block, k_all, preferred_element_type=jnp.float32) * (HEAD_DIM ** -0.5)
    row_ids = row_start + jnp.arange(q_block.shape[0])
    col_ids = jnp.arange(k_all.shape[0])
    scores = jnp.where(row_ids[:, None] >= col_ids[None, :], scores, -jnp.inf)
    return jax.nn.softmax(scores, axis=-1)


def attn_forward(q_grp, k_all, v_all, row_offset):
    n_rows = q_grp.shape[0]
    block_rows = math.gcd(n_rows, 128)
    q_blocks = q_grp.reshape((n_rows // block_rows, block_rows) + q_grp.shape[1:])

    def one_block(block_in):
        q_block, block_idx = block_in
        attn_prob = block_probs(q_block, row_offset + block_idx * block_rows, k_all)
        return jnp.einsum('grqk,kgd->qgrd', attn_prob.astype(jnp.bfloat16), v_all, preferred_element_type=jnp.float32).astype(jnp.bfloat16)

    o_blocks = lax.map(one_block, (q_blocks, jnp.arange(n_rows // block_rows)))
    return o_blocks.reshape(q_grp.shape)


def attn_backward(q_grp, k_all, v_all, do_grp, row_offset):
    n_rows = q_grp.shape[0]
    block_rows = math.gcd(n_rows, 128)
    block_shape = (n_rows // block_rows, block_rows) + q_grp.shape[1:]

    def one_block(carry, block_in):
        dk_acc, dv_acc = carry
        q_block, do_block, block_idx = block_in
        attn_prob = block_probs(q_block, row_offset + block_idx * block_rows, k_all)
        d_prob = jnp.einsum('qgrd,kgd->grqk', do_block, v_all, preferred_element_type=jnp.float32)
        row_dot = jnp.sum(attn_prob * d_prob, axis=-1, keepdims=True)
        d_score = (attn_prob * (d_prob - row_dot) * (HEAD_DIM ** -0.5)).astype(jnp.bfloat16)
        dq_block = jnp.einsum('grqk,kgd->qgrd', d_score, k_all, preferred_element_type=jnp.float32).astype(jnp.bfloat16)
        dk_acc = dk_acc + jnp.einsum('grqk,qgrd->kgd', d_score, q_block, preferred_element_type=jnp.float32)
        dv_acc = dv_acc + jnp.einsum('grqk,qgrd->kgd', attn_prob.astype(jnp.bfloat16), do_block, preferred_element_type=jnp.float32)
        return (dk_acc, dv_acc), dq_block

    zero_acc = jnp.zeros(k_all.shape, jnp.float32)
    kv_sums, dq_blocks = lax.scan(one_block, (zero_acc, zero_acc), (q_grp.reshape(block_shape), do_grp.reshape(block_shape), jnp.arange(block_shape[0])))
    return dq_blocks.reshape(q_grp.shape), kv_sums[0], kv_sums[1]


def solution(mesh):
    sp_size = mesh.shape['sp']
    row_spec = P(('dp', 'sp'), None)
    pos_spec = P(('dp', 'sp'))
    full_spec = P(None, None)
    grad_spec = P('dp', None)

    def local_step(hidden, positions, d_attn, ln_weight, w_q, w_k, w_v, w_o):
        local_rows = hidden.shape[0]
        n_heads = w_q.shape[1] // HEAD_DIM
        kv_heads = w_k.shape[1] // HEAD_DIM
        copies = max(sp_size // kv_heads, 1)
        normed32, norm_vjp = jax.vjp(norm_f32, hidden.astype(jnp.float32), ln_weight.astype(jnp.float32))
        normed = normed32.astype(jnp.bfloat16)
        cos_t, sin_t = rope_tables(positions)
        q_rot = apply_rope(jnp.dot(normed, w_q, preferred_element_type=jnp.float32).reshape(local_rows, n_heads, HEAD_DIM), cos_t, sin_t).astype(jnp.bfloat16)
        k_rot = apply_rope(jnp.dot(normed, w_k, preferred_element_type=jnp.float32).reshape(local_rows, kv_heads, HEAD_DIM), cos_t, sin_t).astype(jnp.bfloat16)
        v_loc = jnp.dot(normed, w_v, preferred_element_type=jnp.float32).astype(jnp.bfloat16).reshape(local_rows, kv_heads, HEAD_DIM)
        if copies > 1:
            k_rot = jnp.repeat(k_rot, copies, axis=1)
            v_loc = jnp.repeat(v_loc, copies, axis=1)
        q_heads = lax.all_to_all(q_rot, 'sp', 1, 0, tiled=True)
        k_heads = lax.all_to_all(k_rot, 'sp', 1, 0, tiled=True)
        v_heads = lax.all_to_all(v_loc, 'sp', 1, 0, tiled=True)
        seq_rows, heads_local = q_heads.shape[0], q_heads.shape[1]
        kv_local = k_heads.shape[1]
        q_grp = q_heads.reshape(seq_rows, kv_local, heads_local // kv_local, HEAD_DIM)
        o_grp = attn_forward(q_grp, k_heads, v_heads, 0)
        o_tok = lax.all_to_all(o_grp.reshape(q_heads.shape), 'sp', 0, 1, tiled=True).reshape(local_rows, n_heads * HEAD_DIM)
        attn_out = jnp.dot(o_tok, w_o, preferred_element_type=jnp.float32).astype(jnp.bfloat16)
        d_o = jnp.einsum('td,ed->te', d_attn, w_o, preferred_element_type=jnp.float32).astype(jnp.bfloat16)
        dw_o = jnp.einsum('te,td->ed', o_tok, d_attn, preferred_element_type=jnp.float32)
        do_heads = lax.all_to_all(d_o.reshape(local_rows, n_heads, HEAD_DIM), 'sp', 1, 0, tiled=True)
        dq_grp, dk_acc, dv_acc = attn_backward(q_grp, k_heads, v_heads, do_heads.reshape(q_grp.shape), 0)
        dq_tok = lax.all_to_all(dq_grp.reshape(q_heads.shape), 'sp', 0, 1, tiled=True)
        dk_tok = lax.all_to_all(dk_acc.astype(jnp.bfloat16), 'sp', 0, 1, tiled=True)
        dv_tok = lax.all_to_all(dv_acc.astype(jnp.bfloat16), 'sp', 0, 1, tiled=True)
        if copies > 1:
            dk_tok = dk_tok.reshape(local_rows, kv_heads, copies, HEAD_DIM).astype(jnp.float32).sum(axis=2).astype(jnp.bfloat16)
            dv_tok = dv_tok.reshape(local_rows, kv_heads, copies, HEAD_DIM).astype(jnp.float32).sum(axis=2).astype(jnp.bfloat16)
        g_q = apply_rope(dq_tok.astype(jnp.float32), cos_t, -sin_t).astype(jnp.bfloat16).reshape(local_rows, n_heads * HEAD_DIM)
        g_k = apply_rope(dk_tok.astype(jnp.float32), cos_t, -sin_t).astype(jnp.bfloat16).reshape(local_rows, kv_heads * HEAD_DIM)
        g_v = dv_tok.reshape(local_rows, kv_heads * HEAD_DIM)
        d_normed = (jnp.einsum('te,de->td', g_q, w_q, preferred_element_type=jnp.float32)
                    + jnp.einsum('te,de->td', g_k, w_k, preferred_element_type=jnp.float32)
                    + jnp.einsum('te,de->td', g_v, w_v, preferred_element_type=jnp.float32))
        dw_q = jnp.einsum('td,te->de', normed, g_q, preferred_element_type=jnp.float32)
        dw_k = jnp.einsum('td,te->de', normed, g_k, preferred_element_type=jnp.float32)
        dw_v = jnp.einsum('td,te->de', normed, g_v, preferred_element_type=jnp.float32)
        d_hid, d_lnw = norm_vjp(d_normed)
        grad_sums = lax.psum((d_lnw, dw_q, dw_k, dw_v, dw_o), 'sp')
        return (attn_out, d_hid.astype(jnp.bfloat16), grad_sums[0].astype(jnp.bfloat16), grad_sums[1].astype(jnp.bfloat16),
                grad_sums[2].astype(jnp.bfloat16), grad_sums[3].astype(jnp.bfloat16), grad_sums[4].astype(jnp.bfloat16))

    return jax.shard_map(local_step, mesh=mesh,
                         in_specs=(row_spec, pos_spec, row_spec, P(None), full_spec, full_spec, full_spec, full_spec),
                         out_specs=(row_spec, row_spec, P('dp'), grad_spec, grad_spec, grad_spec, grad_spec),
                         check_vma=False)
```

profile of v0, /device:TPU:0, one launch (start us, length us, event | category | flops | bytes accessed | tf_op | source)
XLA Modules:
  0.0 3383.4 jit_solution(7090665131844039380)
XLA Ops:
  8.5 9.5 fusion.68
  33.7 22.7 fusion.57
  63.3 24.8 fusion.70
  88.1 10.5 reshape_reshape.19
  98.6 12.7 subtract_convert_fusion.1
  111.4 9.0 pad_maximum_fusion
  132.7 9.2 fusion.58
  143.0 38.6 %all-to-all-done = bf16[512,32,128]{0,2,1:T(8,128)(2,1)} async-done(((bf16[512,32,128]{0,2,1:T(8,128)(2,1)}), bf16[512,32,128]{0,2,1:T(8,128)(2,1)}, u32[]{:S(2)}, u32[]{:S(2)}) %all-to-all-start) | async-done | bytes 4194336 | tf_op jit(solution)/shard_map/all_to_all | solution.py:99
  205.0 645.8 %while.26 = (s32[]{:T(128)}, f32[4096,1,128]{0,2,1:T(8,128)S(1)}, f32[4096,1,128]{0,2,1:T(8,128)}, bf16[32,128,1,4,128]{4,1,0,3,2:T(8,128)(2,1)}, bf16[32,128,1,...) while((s32[]{:T(128)}, f32[4096,1,128]{0,2,1:T(8,128)S(1)}, ...), condition=%wide.region_10.11_spmd.clone, body=%wide.region_6.10_spmd.clone.sunk | while | flops 2724788736 | bytes 101342456 | solution.py:74
  862.8 284.6 %while.25 = (s32[]{:T(128)}, bf16[32,128,1,4,128]{4,1,0,3,2:T(8,128)(2,1)}, s32[32]{0:T(128)S(1)}, bf16[32,128,1,4,128]{4,1,3,2,0:T(8,128)(2,1)}, bf16[4096,1,12...) while((s32[]{:T(128)}, bf16[32,128,1,4,128]{4,1,0,3,2:T(8,128)(2,1)}, ...), condition=%wide.region_5.6_spmd, body=%wide.region_2.5_spmd.sunk | while | flops 1091107968 | bytes 28585088 | solution.py:52
  1155.0 20.6 copy.141
  1205.7 11.2 fusion.61
  1216.9 8.6 fusion.63
  1232.3 17.3 all-to-all-done.5
  1260.4 9.1 copy.143
  1269.5 10.5 reshape.249
  1280.1 12.7 subtract_convert_fusion
  1292.8 10.5 pad_maximum_fusion.1
  1310.5 24.3 fusion.76
  1334.8 26.8 fusion.65
  1372.8 23.6 convolution_convert_fusion.2
  1396.4 30.3 fusion.78
  1426.7 18.6 fusion.54
  1453.5 1929.5 %all-reduce.2 = (bf16[4096]{0:T(1024)(128)(2,1)}, bf16[4096,4096]{1,0:T(8,128)(2,1)}, bf16[4096,1024]{1,0:T(8,128)(2,1)}, bf16[4096,1024]{1,0:T(8,128)(2,1)}, bf16[4096,4096]{1,0:T(8,128)(2,1)}) all-reduce(f32[4096]{0:T(1024)S(1)} %get-tuple-element.197, f32[4096,4096]{1,0:T(8,128)} %fusion.65, ...), channel_id=1, replica_groups=mesh['dp'=1,'sp'=8] {'sp'}, use_global_device_ids=true, to_apply=%region_14.15 | all-reduce | flops 41947136 | bytes 251682816 | tf_op jit(solution)/shard_map/psum | solution.py:128
  (762 shorter events, 1046.3 us)
Async XLA Ops:
  4.5 128.1 %copy-start.18 = (f32[512]{0:T(512)}, f32[512]{0:T(512)S(1)}, u32[]{:S(2)}) copy-start(f32[512]{0:T(512)S(1)} %broadcast_multiply_fusion) | copy-start | bytes 6148
  8.0 124.7 %copy-start.22 = (f32[512]{0:T(512)}, f32[512]{0:T(512)S(1)}, u32[]{:S(2)}) copy-start(f32[512]{0:T(512)S(1)} %fusion.60) | copy-start | bytes 6148
  8.5 124.2 %copy-start.16 = (f32[4096]{0:T(1024)}, f32[4096]{0:T(1024)S(1)}, u32[]{:S(2)}) copy-start(f32[4096]{0:T(1024)S(1)} %convert_element_type.123) | copy-start | bytes 49156
  21.9 76.8 %copy-start.7 = (f32[512,64]{0,1:T(8,128)}, f32[512,64]{0,1:T(8,128)S(1)}, u32[]{:S(2)}) copy-start(f32[512,64]{0,1:T(8,128)S(1)} %get-tuple-element.254) | copy-start | bytes 393220
  29.4 30.2 all-to-all-start.1
  59.6 28.5 copy-start.6
  59.6 69.7 %all-to-all-start.4 = ((bf16[512,32,128]{2,0,1:T(8,128)(2,1)}), bf16[512,32,128]{2,0,1:T(8,128)(2,1)}, u32[]{:S(2)}, u32[]{:S(2)}) async-start(bf16[512,32,128]{2,0,1:T(8,128)(2,1)} %bitcast.257), calls=%async_computation.4 | async-start | bytes 8388608 | tf_op jit(solution)/shard_map/all_to_all | solution.py:110
  129.4 52.3 %all-to-all-start = ((bf16[512,32,128]{0,2,1:T(8,128)(2,1)}), bf16[512,32,128]{0,2,1:T(8,128)(2,1)}, u32[]{:S(2)}, u32[]{:S(2)}) async-start(bf16[512,32,128]{0,2,1:T(8,128)(2,1)} %copy.123), calls=%async_computation | async-start | bytes 8388608 | tf_op jit(solution)/shard_map/all_to_all | solution.py:99
  181.6 20.3 all-to-all-start.2
  856.7 322.2 %all-to-all-start.6 = ((bf16[8,2,32768]{2,1,0:T(2,128)(2,1)}), bf16[8,2,32768]{2,1,0:T(2,128)(2,1)S(1)}, u32[]{:S(2)}, u32[]{:S(2)}) async-start(bf16[8,2,32768]{2,1,0:T(2,128)(2,1)} %reshape.265), calls=%async_computation.6 | async-start | bytes 2097152 | tf_op jit(solution)/shard_map/all_to_all | solution.py:113
  1147.3 28.3 copy-start.11
  1178.9 18.4 all-to-all-start.7
  1190.1 15.5 copy-start.17
  1190.1 15.5 copy-start.19
  1190.1 15.5 copy-start.23
  1197.3 52.3 %all-to-all-start.5 = ((bf16[4096,4,128]{2,1,0:T(4,128)(2,1)}), bf16[4096,4,128]{2,1,0:T(4,128)(2,1)}, u32[]{:S(2)}, u32[]{:S(2)}) async-start(bf16[4096,4,128]{2,1,0:T(4,128)(2,1)} %copy.141), calls=%async_computation.5 | async-start | bytes 8388608 | tf_op jit(solution)/shard_map/all_to_all | solution.py:112
  1205.6 11.2 copy-start.13
  1205.7 19.8 slice-start
  1249.6 112.0 %all-to-all-start.3 = ((bf16[4096,4,128]{2,1,0:T(4,128)(2,1)}), bf16[4096,4,128]{2,1,0:T(4,128)(2,1)}, u32[]{:S(2)}, u32[]{:S(2)}) async-start(bf16[4096,4,128]{2,1,0:T(4,128)(2,1)} %copy.133), calls=%async_computation.3 | async-start | bytes 8388608 | tf_op jit(solution)/shard_map/all_to_all | solution.py:106
  1310.5 24.3 copy-start.2
  1310.5 24.3 copy-start.5
  1396.4 30.3 copy-start.14
  1426.7 18.6 copy-start.21
  1426.7 18.6 copy-start.3
  (73 other events, 331.9 us)
where the time goes:
time: 3400 us; the launch traced here: 3380 us
  blocking collectives  1930 us (57%)
  matrix products  853 us (25%)
  other arithmetic  292 us (9%)
  local copies, waits for them, and re-layouts  172 us (5%)
  waiting for transfers between devices  63 us (2%)
  loops' own time  44.9 us (1%)
    psum x1, blocking collectives, local_step(): grad_sums = lax.psum((d_lnw, dw_q, dw_k, dw_v, dw_o), 'sp')  1930 us
    dot_general x64, matrix products, block_probs(): jnp.einsum('qgrd,kgd->grqk', q_block, k_all, preferred_element_type=jnp.f...  170 us
    dot_general x32, matrix products, one_block(): jnp.einsum('qgrd,kgd->grqk', do_block, v_all, preferred_element_type=jnp....  137 us
    another operation x36, other arithmetic  136 us
    dot_general x32, matrix products, one_block(): jnp.einsum('grqk,kgd->qgrd', attn_prob.astype(jnp.bfloat16), v_all, prefe...  109 us
    dot_general x32, matrix products, one_block(): jnp.einsum('grqk,qgrd->kgd', attn_prob.astype(jnp.bfloat16), do_block, pr...  94.6 us
    reduce_sum x64, other arithmetic, block_probs(): return jax.nn.softmax(scores, axis=-1)  82.1 us
  transfers between devices with their start and end apart: 8, of which 3 were waited for; matrix products, arithmetic and copies ran while one was open for 17% of the time, Pallas kernels for 0%

commit v1 on v0

v1 whole, which is shorter than its diff:
```python
import functools
import jax
import jax.numpy as jnp
from jax import lax
from jax.experimental import pallas as pl
from jax.experimental.pallas import tpu as pltpu
from jax.sharding import PartitionSpec as P

HEAD_DIM = 128
LN_EPS = 1e-5
ROPE_BASE = 10000.0
SCALE = HEAD_DIM ** -0.5
LOG2E = 1.4426950408889634
VMEM_LIMIT = 67_000_000
BF16 = jnp.bfloat16
F32 = jnp.float32


def norm_f32(hid_f32, weight_f32):
    mean_val = jnp.mean(hid_f32, axis=-1, keepdims=True)
    centered = hid_f32 - mean_val
    var_val = jnp.mean(centered * centered, axis=-1, keepdims=True)
    return centered * lax.rsqrt(var_val + LN_EPS) * weight_f32


def rope_tables(positions):
    inv_freq = ROPE_BASE ** (-jnp.arange(0, HEAD_DIM, 2, dtype=F32) / HEAD_DIM)
    angles = positions.astype(F32)[:, None] * inv_freq[None, :]
    cos_t = jnp.repeat(jnp.cos(angles), 2, axis=1)
    sin_t = jnp.repeat(jnp.sin(angles), 2, axis=1)
    sign = jnp.where(jnp.arange(HEAD_DIM) % 2 == 0, -1.0, 1.0).astype(F32)
    return cos_t, sin_t * sign[None, :]


def rotate(x, cos_t, sin_t):
    lane = lax.broadcasted_iota(jnp.int32, x.shape, 1)
    swapped = jnp.where(lane % 2 == 0, pltpu.roll(x, HEAD_DIM - 1, 1), pltpu.roll(x, 1, 1))
    return x * cos_t + swapped * sin_t


def qkv_kernel(dev_ref, h_ref, wq_ref, wk_ref, wv_ref, cos_ref, sin_ref, q_ref, k_ref, kt_ref, v_ref, vt_ref):
    h = h_ref[...]
    cos_t, sin_t = cos_ref[...], sin_ref[...]
    for n in range(q_ref.shape[1] // HEAD_DIM):
        cols = slice(n * HEAD_DIM, (n + 1) * HEAD_DIM)
        q_ref[:, cols] = rotate(jnp.dot(h, wq_ref[:, cols], preferred_element_type=F32), cos_t, sin_t).astype(BF16)
    k = rotate(jnp.dot(h, wk_ref[...], preferred_element_type=F32), cos_t, sin_t)
    k_ref[...] = k.astype(BF16)
    kt_ref[...] = k.T.astype(BF16)
    v = jnp.dot(h, wv_ref[...], preferred_element_type=F32)
    v_ref[...] = v.astype(BF16)
    vt_ref[...] = v.T.astype(BF16)


def qkv_proj(dev, h_all, w_q, w_k, w_v, cos_t, sin_t, width, bm=512):
    seq, feat = h_all.shape
    rows = lambda i, d: (i, 0)
    cols = lambda i, d: (0, i)
    mine = lambda i, d: (0, d[0])
    return pl.pallas_call(
        qkv_kernel,
        grid_spec=pltpu.PrefetchScalarGridSpec(
            num_scalar_prefetch=1, grid=(seq // bm,),
            in_specs=[pl.BlockSpec((bm, feat), rows), pl.BlockSpec((feat, width), mine), pl.BlockSpec((feat, HEAD_DIM), mine),
                      pl.BlockSpec((feat, HEAD_DIM), mine), pl.BlockSpec((bm, HEAD_DIM), rows), pl.BlockSpec((bm, HEAD_DIM), rows)],
            out_specs=[pl.BlockSpec((bm, width), rows), pl.BlockSpec((bm, HEAD_DIM), rows), pl.BlockSpec((HEAD_DIM, bm), cols),
                       pl.BlockSpec((bm, HEAD_DIM), rows), pl.BlockSpec((HEAD_DIM, bm), cols)]),
        out_shape=[jax.ShapeDtypeStruct((seq, width), BF16), jax.ShapeDtypeStruct((seq, HEAD_DIM), BF16),
                   jax.ShapeDtypeStruct((HEAD_DIM, seq), BF16), jax.ShapeDtypeStruct((seq, HEAD_DIM), BF16),
                   jax.ShapeDtypeStruct((HEAD_DIM, seq), BF16)],
        compiler_params=pltpu.CompilerParams(vmem_limit_bytes=VMEM_LIMIT),
        cost_estimate=pl.CostEstimate(flops=2 * seq * feat * (width + 256), bytes_accessed=seq * feat * 2, transcendentals=0),
        name="qkv_proj")(dev, h_all, w_q, w_k, w_v, cos_t, sin_t)


def do_kernel(dev_ref, g_ref, wo_ref, do_ref):
    do_ref[...] = lax.dot_general(g_ref[...], wo_ref[...], (((1,), (1,)), ((), ())), preferred_element_type=F32).astype(BF16)


def do_proj(dev, g_all, w_o, width, bm=512):
    seq, feat = g_all.shape
    return pl.pallas_call(
        do_kernel,
        grid_spec=pltpu.PrefetchScalarGridSpec(
            num_scalar_prefetch=1, grid=(seq // bm,),
            in_specs=[pl.BlockSpec((bm, feat), lambda i, d: (i, 0)), pl.BlockSpec((width, feat), lambda i, d: (d[0], 0))],
            out_specs=pl.BlockSpec((bm, width), lambda i, d: (i, 0))),
        out_shape=jax.ShapeDtypeStruct((seq, width), BF16),
        compiler_params=pltpu.CompilerParams(vmem_limit_bytes=VMEM_LIMIT),
        cost_estimate=pl.CostEstimate(flops=2 * seq * feat * width, bytes_accessed=seq * feat * 2, transcendentals=0),
        name="do_proj")(dev, g_all, w_o)


def stack_heads(x):
    return jnp.concatenate([x[:, n * HEAD_DIM:(n + 1) * HEAD_DIM] for n in range(x.shape[1] // HEAD_DIM)], axis=0)


def unstack_heads(ref, x, rows):
    for n in range(x.shape[0] // rows):
        ref[:, n * HEAD_DIM:(n + 1) * HEAD_DIM] = x[n * rows:(n + 1) * rows].astype(ref.dtype)


def causal(shape, bq, offset):
    rows = lax.rem(lax.broadcasted_iota(jnp.int32, shape, 0), bq) + offset
    return rows >= lax.broadcasted_iota(jnp.int32, shape, 1)


def fwd_kernel(bq, bk, q_ref, kt_ref, v_ref, o_ref, lse_ref, s_scr):
    qi = pl.program_id(0)
    q = stack_heads(q_ref[...])
    rows = q.shape[0]
    nfull = (qi * bq) // bk

    def scores(j):
        return jnp.dot(q, kt_ref[:, pl.ds(pl.multiple_of(j * bk, bk), bk)], preferred_element_type=F32) * (SCALE * LOG2E)

    def lane_max(m, s):
        for c in range(bk // 128):
            m = jnp.maximum(m, s[:, c * 128:(c + 1) * 128])
        return m

    def score_step(j, m):
        s = scores(j)
        s_scr[j] = s
        return lane_max(m, s)

    m = lax.fori_loop(0, nfull, score_step, jnp.full((rows, 128), -jnp.inf, F32))
    s = jnp.where(causal((rows, bk), bq, qi * bq - nfull * bk), scores(nfull), -jnp.inf)
    s_scr[nfull] = s
    m = jnp.max(lane_max(m, s), axis=1, keepdims=True)

    def value_step(j, carry):
        l, o = carry
        p = jnp.exp2(s_scr[j] - m)
        for t in range(bk // 128):
            l = l + p[:, t * 128:(t + 1) * 128]
        o = o + jnp.dot(p.astype(BF16), v_ref[pl.ds(pl.multiple_of(j * bk, bk), bk), :], preferred_element_type=F32)
        return l, o

    l, o = lax.fori_loop(0, nfull + 1, value_step, (jnp.zeros((rows, 128), F32), jnp.zeros((rows, HEAD_DIM), F32)))
    l = jnp.sum(l, axis=1, keepdims=True)
    unstack_heads(o_ref, o / l, bq)
    lse_ref[...] = (m + jnp.log2(l)).reshape(lse_ref.shape)


def attn_forward(q, kt, v, bq=256, bk=1024):
    seq, width = q.shape
    heads = width // HEAD_DIM
    return pl.pallas_call(
        functools.partial(fwd_kernel, bq, bk), grid=(seq // bq,),
        in_specs=[pl.BlockSpec((bq, width), lambda i: (i, 0)), pl.BlockSpec((HEAD_DIM, seq), lambda i: (0, 0)),
                  pl.BlockSpec((seq, HEAD_DIM), lambda i: (0, 0))],
        out_specs=[pl.BlockSpec((bq, width), lambda i: (i, 0)), pl.BlockSpec((heads, bq, 1), lambda i: (0, i, 0))],
        out_shape=[jax.ShapeDtypeStruct((seq, width), BF16), jax.ShapeDtypeStruct((heads, seq, 1), F32)],
        scratch_shapes=[pltpu.VMEM((seq // bk, heads * bq, bk), F32)],
        compiler_params=pltpu.CompilerParams(vmem_limit_bytes=VMEM_LIMIT),
        cost_estimate=pl.CostEstimate(flops=8 * seq * seq * width, bytes_accessed=seq * width * 8, transcendentals=0),
        name="attn_fwd")(q, kt, v)


def bwd_kernel(bq, bk, q_ref, do_ref, lse_ref, k_ref, kt_ref, vt_ref, cos_ref, sin_ref, gq_ref, gk_ref, gv_ref, p_scr, dp_scr, dkt_scr, dvt_scr):
    qi = pl.program_id(0)
    q = stack_heads(q_ref[...])
    do = stack_heads(do_ref[...])
    rows = q.shape[0]
    lse = lse_ref[...].reshape(rows, 1)
    q_t = q.T
    do_t = do.T
    nfull = (qi * bq) // bk

    @pl.when(qi == 0)
    def _():
        dkt_scr[...] = jnp.zeros_like(dkt_scr)
        dvt_scr[...] = jnp.zeros_like(dvt_scr)

    def prob_step(j, r, masked):
        sl = pl.ds(pl.multiple_of(j * bk, bk), bk)
        s = jnp.dot(q, kt_ref[:, sl], preferred_element_type=F32) * (SCALE * LOG2E)
        p = jnp.exp2(s - lse)
        if masked:
            p = jnp.where(causal((rows, bk), bq, qi * bq - nfull * bk), p, 0.0)
        dp = jnp.dot(do, vt_ref[:, sl], preferred_element_type=F32)
        pd = p * dp
        for t in range(bk // 128):
            r = r + pd[:, t * 128:(t + 1) * 128]
        p_scr[j] = p
        dp_scr[j] = dp
        dvt_scr[:, sl] += jnp.dot(do_t, p.astype(BF16), preferred_element_type=F32)
        return r

    r = lax.fori_loop(0, nfull, lambda j, r: prob_step(j, r, False), jnp.zeros((rows, 128), F32))
    r = prob_step(nfull, r, True)
    r = jnp.sum(r, axis=1, keepdims=True)

    def grad_step(j, dq):
        sl = pl.ds(pl.multiple_of(j * bk, bk), bk)
        ds = (p_scr[j] * (dp_scr[j] - r) * SCALE).astype(BF16)
        dkt_scr[:, sl] += jnp.dot(q_t, ds, preferred_element_type=F32)
        return dq + jnp.dot(ds, k_ref[sl, :], preferred_element_type=F32)

    dq = lax.fori_loop(0, nfull + 1, grad_step, jnp.zeros((rows, HEAD_DIM), F32))
    dq = dq.astype(BF16).astype(F32)
    start = pl.ds(pl.multiple_of(qi * bq, bq), bq)
    cos_t, sin_t = cos_ref[start, :], sin_ref[start, :]
    for n in range(rows // bq):
        gq_ref[:, n * HEAD_DIM:(n + 1) * HEAD_DIM] = rotate(dq[n * bq:(n + 1) * bq], cos_t, -sin_t).astype(BF16)

    @pl.when(qi == pl.num_programs(0) - 1)
    def _():
        dk = dkt_scr[...].T.astype(BF16).astype(F32)
        gk_ref[...] = rotate(dk, cos_ref[...], -sin_ref[...]).astype(BF16)
        gv_ref[...] = dvt_scr[...].T.astype(BF16)


def attn_backward(q, do, lse, k, kt, vt, cos_t, sin_t, bq=256, bk=512):
    seq, width = q.shape
    heads = width // HEAD_DIM
    tile = pl.BlockSpec((bq, width), lambda i: (i, 0))
    tall = pl.BlockSpec((seq, HEAD_DIM), lambda i: (0, 0))
    wide = pl.BlockSpec((HEAD_DIM, seq), lambda i: (0, 0))
    return pl.pallas_call(
        functools.partial(bwd_kernel, bq, bk), grid=(seq // bq,),
        in_specs=[tile, tile, pl.BlockSpec((heads, bq, 1), lambda i: (0, i, 0)), tall, wide, wide, tall, tall],
        out_specs=[tile, tall, tall],
        out_shape=[jax.ShapeDtypeStruct((seq, width), BF16), jax.ShapeDtypeStruct((seq, HEAD_DIM), BF16),
                   jax.ShapeDtypeStruct((seq, HEAD_DIM), BF16)],
        scratch_shapes=[pltpu.VMEM((seq // bk, heads * bq, bk), F32), pltpu.VMEM((seq // bk, heads * bq, bk), F32),
                        pltpu.VMEM((HEAD_DIM, seq), F32), pltpu.VMEM((HEAD_DIM, seq), F32)],
        compiler_params=pltpu.CompilerParams(vmem_limit_bytes=VMEM_LIMIT),
        cost_estimate=pl.CostEstimate(flops=16 * seq * seq * width, bytes_accessed=seq * width * 8, transcendentals=0),
        name="attn_bwd")(q, do, lse, k, kt, vt, cos_t, sin_t)


def solution(mesh):
    sp_size = mesh.shape['sp']
    pairs = [[i, i + 1] for i in range(0, sp_size, 2)]
    row_spec = P(('dp', 'sp'), None)
    pos_spec = P(('dp', 'sp'))
    full_spec = P(None, None)
    grad_spec = P('dp', None)

    def local_step(hidden, positions, d_attn, ln_weight, w_q, w_k, w_v, w_o):
        dev = lax.axis_index('sp')
        core = lax.rem(dev, 2)
        dev1 = dev.reshape(1)
        local_rows, feat = hidden.shape
        seq = local_rows * sp_size
        width = w_q.shape[1] // sp_size
        kv_width = w_k.shape[1] // sp_size
        normed32, norm_vjp = jax.vjp(norm_f32, hidden.astype(F32), ln_weight.astype(F32))
        normed = normed32.astype(BF16)
        pos_all = lax.all_gather(positions, 'sp', axis=0, tiled=True)
        h_all = lax.all_gather(normed, 'sp', axis=0, tiled=True)
        g_all = lax.all_gather(d_attn, 'sp', axis=0, tiled=True)
        cos_t, sin_t = rope_tables(pos_all)
        q, k, kt, v, vt = qkv_proj(dev1, h_all, w_q, w_k, w_v, cos_t, sin_t, width)
        o, lse = attn_forward(q, kt, v)
        o_all = lax.all_gather(o, 'sp', axis=0)
        do = do_proj(dev1, g_all, w_o, width)
        gq, gk, gv = attn_backward(q, do, lse, k, kt, vt, cos_t, sin_t)
        gq_all = lax.all_gather(gq, 'sp', axis=0)
        gk_all = lax.all_gather(gk, 'sp', axis=0)
        gv_all = lax.all_gather(gv, 'sp', axis=0)

        def own_rows(x_all):
            x = lax.dynamic_slice_in_dim(x_all, dev * local_rows, local_rows, axis=1)
            return jnp.transpose(x, (1, 0, 2)).reshape(local_rows, -1)

        def half(x_all):
            n = sp_size // 2
            return lax.dynamic_slice_in_dim(x_all, core * n, n, axis=0)

        attn_out = jnp.dot(own_rows(o_all), w_o, preferred_element_type=F32).astype(BF16)
        dw_o = jnp.einsum('ste,td->sed', half(o_all), g_all, preferred_element_type=F32).astype(BF16)
        dw_o = lax.all_gather(dw_o.reshape(-1, feat), 'sp', axis=0, tiled=True, axis_index_groups=pairs)

        def grad_in(x_all):
            x = half(x_all)
            y = jnp.einsum('td,ste->dse', h_all, x, preferred_element_type=F32).astype(BF16)
            return lax.all_gather(y.reshape(feat, -1), 'sp', axis=1, tiled=True, axis_index_groups=pairs)

        dw_q, dw_k, dw_v = grad_in(gq_all), grad_in(gk_all), grad_in(gv_all)
        d_normed = (jnp.einsum('te,de->td', own_rows(gq_all), w_q, preferred_element_type=F32)
                    + jnp.einsum('te,de->td', own_rows(gk_all), w_k, preferred_element_type=F32)
                    + jnp.einsum('te,de->td', own_rows(gv_all), w_v, preferred_element_type=F32))
        d_hid, d_lnw = norm_vjp(d_normed)
        d_lnw = lax.psum(d_lnw, 'sp')
        return (attn_out, d_hid.astype(BF16), d_lnw.astype(BF16), dw_q, dw_k, dw_v, dw_o)

    return jax.shard_map(local_step, mesh=mesh,
                         in_specs=(row_spec, pos_spec, row_spec, P(None), full_spec, full_spec, full_spec, full_spec),
                         out_specs=(row_spec, row_spec, P('dp'), grad_spec, grad_spec, grad_spec, grad_spec),
                         check_vma=False)
```

time: 3400 us -> 1230 us (0.36)
  blocking collectives: 1930 us -> 35.8 us
  matrix products: 853 us -> 278 us
  waiting for transfers between devices: 63 us -> 391 us
  Pallas kernels: 0 us -> 308 us
  other arithmetic: 292 us -> 30.5 us
  loops' own time: 44.9 us -> 0 us
    psum x1, blocking collectives: 1930 us -> 22.3 us  [local_step(): d_lnw = lax.psum(d_lnw, 'sp')]
    dot_general x236 -> x6, matrix products: 853 us -> 233 us  [the longest x1 79.9 us: local_step(): jnp.einsum('ste,td->sed', half(o_all), g_all, preferred_element_type=F32)]
    all_gather x0 -> x10, waiting for transfers between devices: none -> 389 us  [the longest x1 124 us: local_step(): h_all = lax.all_gather(normed, 'sp', axis=0, tiled=True)]
    pallas_call x0 -> x4, Pallas kernels: none -> 308 us  [the longest x1 146 us: attn_backward(): pl.pallas_call(functools.partial(bwd_kernel, bq, bk), grid=(seq // bq,),...]
    another operation x40 -> x0, other arithmetic: 160 us -> none
    reduce_sum x64 -> x0, other arithmetic: 82.1 us -> none  [block_probs(): return jax.nn.softmax(scores, axis=-1)]
    unnamed x57 -> x36, local copies, waits for them, and re-layouts: 9.63 us -> 90.1 us
    all_to_all x8 -> x0, waiting for transfers between devices: 63 us -> none  [the longest x1 38.6 us: local_step(): q_heads = lax.all_to_all(q_rot, 'sp', 1, 0, tiled=True)]
  transfers between devices with their start and end apart: 8 -> 10, of which waited for: 3 -> 6; matrix products, arithmetic and copies ran while one was open for 17% -> 32% of each run, Pallas kernels for 0% -> 11%
where the time goes in v1:
time: 1230 us; the launch traced here: 1220 us
  waiting for transfers between devices  391 us (32%)
  Pallas kernels  308 us (25%)
  matrix products  278 us (23%)
  local copies, waits for them, and re-layouts  158 us (13%)
  blocking collectives  35.8 us (3%)
  other arithmetic  30.5 us (2%)
  between operations  14.8 us (1%)
    pallas_call x1, Pallas kernels, attn_backward(): pl.pallas_call(functools.partial(bwd_kernel, bq, bk), grid=(seq // bq,),...  146 us
    all_gather x1, waiting for transfers between devices, local_step(): h_all = lax.all_gather(normed, 'sp', axis=0, tiled=True)  124 us
    unnamed x36, local copies, waits for them, and re-layouts  90.1 us
    dot_general x1, matrix products, local_step(): jnp.einsum('ste,td->sed', half(o_all), g_all, preferred_element_type=F32)  79.9 us
    pallas_call x1, Pallas kernels, attn_forward(): pl.pallas_call(functools.partial(fwd_kernel, bq, bk), grid=(seq // bq,),...  79.3 us
    dot_general x1, matrix products, grad_in(): jnp.einsum('td,ste->dse', h_all, x, preferred_element_type=F32).astype(BF16)  78.9 us
    all_gather x1, waiting for transfers between devices, local_step(): gq_all = lax.all_gather(gq, 'sp', axis=0)  77.5 us
    all_gather x1, waiting for transfers between devices, local_step(): o_all = lax.all_gather(o, 'sp', axis=0)  73.4 us
  transfers between devices with their start and end apart: 10, of which 6 were waited for; matrix products, arithmetic and copies ran while one was open for 32% of the time, Pallas kernels for 11%

profile of v1, /device:TPU:0, one launch (start us, length us, event | category | flops | bytes accessed | tf_op | source)
XLA Modules:
  0.0 1217.5 jit_solution(1427206929466170994)
XLA Ops:
  20.6 13.6 %all-gather.4 = s32[8,1,512]{2,1,0:T(1,128)S(1)} all-gather(s32[1,1,512]{2,1,0:T(1,128)S(1)} %bitcast.80), channel_id=1, replica_groups=mesh['dp'=1,'sp'=8] {'sp'}, dimensions={0}, use_global_device_ids=true | all-gather | bytes 18432 | tf_op jit(solution)/shard_map/all_gather | solution.py:252
  54.2 123.8 %all-gather.16.cloned.1.call-done.h_ref = bf16[4096,4096]{1,0:T(8,128)(2,1)} async-done(((bf16[512,4096]{1,0:T(8,128)(2,1)}), bf16[4096,4096]{1,0:T(8,128)(2,1)}) %all-gather.16.cloned.1.call-update) | async-done | bytes 33554448 | tf_op jit(solution)/shard_map/all_gather | solution.py:253
  178.0 60.0 %qkv_proj.1 = (bf16[4096,512]{1,0:T(8,128)(2,1)}, bf16[4096,128]{1,0:T(8,128)(2,1)}, bf16[128,4096]{1,0:T(8,128)(2,1)}, bf16[4096,128]{1,0:T(8,128)(2,1)}, bf16[128,4096]{1,0:T(8,128)(2,1)}) custom-call(s32[1]{0:T(128)} %bitcast.dev_ref, bf16[4096,4096]{1,0:T(8,128)(2,1)} %all-gather.16.cloned.1.call-done.h_ref, bf16[4096,4096]{1,0:T(8,128)(2,1)} %wq_ref.1, ...), custom_call_target="tpu_custom_call" | custom-call | flops 25769803776 | bytes 33554432 | tf_op jit(solution)/shard_map/qkv_proj/pallas_call | solution.py:60
  238.0 79.3 %attn_fwd.1 = (bf16[4096,512]{1,0:T(8,128)(2,1)}, f32[4,4096,1]{2,1,0:T(8,128)}) custom-call(bf16[4096,512]{1,0:T(8,128)(2,1)} %get-tuple-element.17.q_ref, bf16[128,4096]{1,0:T(8,128)(2,1)} %get-tuple-element.18.kt_ref, bf16[4096,128]{1,0:T(8,128)(2,1)} %get-tuple-element.19.v_ref), custom_call_target="tpu_custom_call" | custom-call | flops 68719476736 | bytes 16777216 | tf_op jit(solution)/shard_map/attn_fwd/pallas_call | solution.py:149
  317.4 17.7 %all-gather.18.cloned.1.call-done.g_ref = bf16[4096,4096]{1,0:T(8,128)(2,1)} async-done(((bf16[512,4096]{1,0:T(8,128)(2,1)}), bf16[4096,4096]{1,0:T(8,128)(2,1)}) %all-gather.18.cloned.1.call-update) | async-done | bytes 33554448 | tf_op jit(solution)/shard_map/all_gather | solution.py:254
  335.1 23.5 %do_proj.1.do_ref = bf16[4096,512]{1,0:T(8,128)(2,1)} custom-call(s32[1]{0:T(128)} %bitcast.dev_ref, bf16[4096,4096]{1,0:T(8,128)(2,1)} %all-gather.18.cloned.1.call-done.g_ref, bf16[4096,4096]{1,0:T(8,128)(2,1)} %wo_ref.1), custom_call_target="tpu_custom_call" | custom-call | flops 17179869184 | bytes 33554432 | tf_op jit(solution)/shard_map/do_proj/pallas_call | solution.py:82
  358.6 145.5 %attn_bwd.1 = (bf16[4096,512]{1,0:T(8,128)(2,1)}, bf16[4096,128]{1,0:T(8,128)(2,1)}, bf16[4096,128]{1,0:T(8,128)(2,1)}) custom-call(bf16[4096,512]{1,0:T(8,128)(2,1)} %get-tuple-element.17.q_ref, bf16[4096,512]{1,0:T(8,128)(2,1)} %do_proj.1.do_ref, f32[4,4096,1]{2,1,0:T(8,128)} %get-tuple-element.21.lse_ref, bf16[4096,128]{1,0:T(8,128)(2,1)} %get-tuple-element.22.k_ref, ...), custom_call_target="tpu_custom_call" | custom-call | flops 137438953472 | bytes 16777216 | tf_op jit(solution)/shard_map/attn_bwd/pallas_call | solution.py:221
  505.9 46.7 %all-gather.32.cloned.1.call-done = bf16[32768,128]{1,0:T(8,128)(2,1)} async-done(((bf16[4096,128]{1,0:T(8,128)(2,1)}), bf16[32768,128]{1,0:T(8,128)(2,1)}) %all-gather.32.cloned.1.call-update) | async-done | bytes 8388624 | tf_op jit(solution)/shard_map/all_gather | solution.py:262
  552.6 50.0 %all-gather.34.cloned.1.call-done = bf16[32768,128]{1,0:T(8,128)(2,1)} async-done(((bf16[4096,128]{1,0:T(8,128)(2,1)}), bf16[32768,128]{1,0:T(8,128)(2,1)}) %all-gather.34.cloned.1.call-update) | async-done | bytes 8388624 | tf_op jit(solution)/shard_map/all_gather | solution.py:263
  616.5 22.6 %fusion.33 = f32[4096,512]{0,1:S(1)} fusion(bf16[4096,512]{0,1:T(8,128)(2,1)} %bitcast.66, bf16[4096,4096]{1,0:T(8,128)(2,1)} %all-gather.16.cloned.1.call-done.h_ref), kind=kOutput, calls=%fused_computation.47 | convolution fusion | flops 17179869184 | bytes 46137344
  655.0 22.6 %fusion.32 = f32[4096,512]{0,1:S(1)} fusion(bf16[4096,512]{0,1:T(8,128)(2,1)} %bitcast.67, bf16[4096,4096]{1,0:T(8,128)(2,1)} %all-gather.16.cloned.1.call-done.h_ref), kind=kOutput, calls=%fused_computation.46 | convolution fusion | flops 17179869184 | bytes 46137344
  686.8 73.4 %all-gather.28.cloned.1.call-done = bf16[32768,512]{1,0:T(8,128)(2,1)} async-done(((bf16[4096,512]{1,0:T(8,128)(2,1)}), bf16[32768,512]{1,0:T(8,128)(2,1)}) %all-gather.28.cloned.1.call-update) | async-done | bytes 33554448 | tf_op jit(solution)/shard_map/all_gather | solution.py:258
  760.1 79.9 %fusion.11 = bf16[4,512,4096]{2,1,0:T(8,128)(2,1)} fusion(bf16[4096,4096]{1,0:T(8,128)(2,1)} %all-gather.18.cloned.1.call-done.g_ref, bf16[8,4096,512]{2,1,0:T(8,128)(2,1)} %bitcast.75, s32[]{:T(128)S(6)} %select_n.34), kind=kOutput, calls=%fused_computation.8 | convolution fusion | flops 68727865344 | bytes 67108864 | tf_op jit(solution)/shard_map/ste,td->sed/dot_general | solution.py:274
  840.1 77.5 %all-gather.30.cloned.1.call-done = bf16[32768,512]{1,0:T(8,128)(2,1)} async-done(((bf16[4096,512]{1,0:T(8,128)(2,1)}), bf16[32768,512]{1,0:T(8,128)(2,1)}) %all-gather.30.cloned.1.call-update) | async-done | bytes 33554448 | tf_op jit(solution)/shard_map/all_gather | solution.py:261
  917.6 78.9 %fusion.6 = bf16[4096,4,512]{0,2,1:T(8,128)(2,1)} fusion(bf16[8,4096,512]{2,1,0:T(8,128)(2,1)} %bitcast.77, s32[]{:T(128)S(6)} %select_n.34, bf16[4096,4096]{1,0:T(8,128)(2,1)} %all-gather.16.cloned.1.call-done.h_ref), kind=kOutput, calls=%fused_computation.7 | convolution fusion | flops 68727865344 | bytes 67108864 | tf_op jit(solution)/shard_map/td,ste->dse/dot_general | solution.py:279
  996.5 22.4 %copy.44 = bf16[4096,2048]{1,0:T(8,128)(2,1)} copy(bf16[4096,2048]{0,1:T(8,128)(2,1)} %bitcast.62) | data formatting | bytes 33554432 | tf_op jit(solution)/shard_map/reshape | solution.py:280
  1021.8 10.5 fusion.31
  1054.2 24.3 %fusion.30 = f32[512,4096]{1,0:T(8,128)} fusion(bf16[512,4096]{0,1:T(8,128)(2,1)} %bitcast.68, bf16[4096,4096]{1,0:T(8,128)(2,1)} %wq_ref.1), kind=kOutput, calls=%fused_computation.44 | convolution fusion | flops 17179869184 | bytes 46137344 | tf_op jit(solution)/shard_map/te,de->td/dot_general | solution.py:283
  1078.5 15.8 %fusion.23 = (f32[4096]{0:T(1024)S(1)}, f32[512]{0:T(512)S(1)}, f32[512,4096]{1,0:T(8,128)}) fusion(bf16[512,4096]{1,0:T(8,128)(2,1)S(1)} %copy-done.1, f32[512]{0:T(512)S(1)} %copy-done.10, f32[512]{0:T(512)S(1)} %copy-done.6, f32[4096]{0:T(1024)S(1)} %copy-done.4, bf16[512,1024]{0,1:T(8,128)(2,1)S(1)} %bitcast.73, bf16[4096,1024]{1,0:T(8,128)(2,1)} %wv_ref.1, ...), kind=kOutput, calls=%fused_computation.18 | convolution fusion | flops 4315934208 | bytes 38836224 | tf_op jit(solution)/shard_map/te,de->td/dot_general | solution.py:285
  1094.2 22.3 %psum.7 = bf16[4096]{0:T(1024)(128)(2,1)} all-reduce(f32[4096]{0:T(1024)S(1)} %get-tuple-element.27), channel_id=1, replica_groups=mesh['dp'=1,'sp'=8] {'sp'}, use_global_device_ids=true, to_apply=%region_5.6 | all-reduce | flops 4096 | bytes 24576 | tf_op jit(solution)/shard_map/psum | solution.py:287
  1125.8 23.1 %convolution_convert_fusion = bf16[512,4096]{1,0:T(8,128)(2,1)} fusion(bf16[512,4096]{0,1:T(8,128)(2,1)S(1)} %bitcast.65, bf16[4096,4096]{1,0:T(8,128)(2,1)} %wo_ref.1), kind=kOutput, calls=%fused_computation.23 | convolution fusion | flops 17181966336 | bytes 41943040 | tf_op jit(solution)/shard_map/dot_general | solution.py:273
  1148.9 22.9 %copy.62 = bf16[4096,4096]{1,0:T(8,128)(2,1)} copy(bf16[4096,4096]{1,0:T(8,128)(2,1)} %all-gather.20.cloned.1.call-done) | data formatting | bytes 67108864
  1171.8 7.8 copy.63
  1187.3 22.9 %copy.65 = bf16[4096,4096]{1,0:T(8,128)(2,1)} copy(bf16[4096,4096]{1,0:T(8,128)(2,1)} %all-gather.26.cloned.1.call-done) | data formatting | bytes 67108864
  (86 shorter events, 115.6 us)
Async XLA Ops:
  7.2 7.1 copy-start.11
  7.2 170.8 %all-gather.16.cloned.1.call-start = ((), (), s32[]{:S(2)}) async-start(), calls=%async_computation | async-start | bytes 37748736 | tf_op jit(solution)/shard_map/all_gather | solution.py:253
  7.2 8.2 copy-start
  10.2 4.0 copy-start.5
  13.6 0.6 copy-start.7
  14.2 0.6 copy-start.9
  14.8 0.6 copy-start.3
  15.4 5.2 copy-start.12
  19.8 315.3 %all-gather.18.cloned.1.call-start = ((), (), s32[]{:S(2)}) async-start(), calls=%async_computation.1 | async-start | bytes 37748736 | tf_op jit(solution)/shard_map/all_gather | solution.py:254
  20.6 532.0 %all-gather.32.cloned.1.call-start = ((), (), s32[]{:S(2)}) async-start(), calls=%async_computation.8 | async-start | bytes 9437184 | tf_op jit(solution)/shard_map/all_gather | solution.py:262
  504.1 98.5 %all-gather.34.cloned.1.call-start = ((), (), s32[]{:S(2)}) async-start(), calls=%async_computation.9 | async-start | bytes 9437184 | tf_op jit(solution)/shard_map/all_gather | solution.py:263
  504.7 255.4 %all-gather.28.cloned.1.call-start = ((), (), s32[]{:S(2)}) async-start(), calls=%async_computation.6 | async-start | bytes 37748736 | tf_op jit(solution)/shard_map/all_gather | solution.py:258
  505.3 412.3 %all-gather.30.cloned.1.call-start = ((), (), s32[]{:S(2)}) async-start(), calls=%async_computation.7 | async-start | bytes 37748736 | tf_op jit(solution)/shard_map/all_gather | solution.py:261
  505.9 526.5 %all-gather.24.cloned.1.call-start = ((), (), s32[]{:S(2)}) async-start(), calls=%async_computation.4 | async-start | bytes 12582912 | tf_op jit(solution)/shard_map/all_gather | solution.py:280
  648.2 384.1 %all-gather.22.cloned.1.call-start = ((), (), s32[]{:S(2)}) async-start(), calls=%async_computation.3 | async-start | bytes 12582912 | tf_op jit(solution)/shard_map/all_gather | solution.py:280
  686.7 462.2 %all-gather.26.cloned.1.call-start = ((), (), s32[]{:S(2)}) async-start(), calls=%async_computation.5 | async-start | bytes 50331648 | tf_op jit(solution)/shard_map/all_gather | solution.py:275
  840.1 308.8 %all-gather.20.cloned.1.call-start = ((), (), s32[]{:S(2)}) async-start(), calls=%async_computation.2 | async-start | bytes 50331648 | tf_op jit(solution)/shard_map/all_gather | solution.py:280
  1054.2 24.3 %copy-start.1 = (bf16[512,4096]{1,0:T(8,128)(2,1)S(1)}, bf16[512,4096]{1,0:T(8,128)(2,1)}, u32[]{:S(2)}) copy-start(bf16[512,4096]{1,0:T(8,128)(2,1)} %param.8) | copy-start | bytes 12582916
  1054.2 24.3 %copy-start.4 = (f32[4096]{0:T(1024)S(1)}, f32[4096]{0:T(1024)}, u32[]{:S(2)}) copy-start(f32[4096]{0:T(1024)} %copy-done.3) | copy-start | bytes 49156
  1054.2 24.3 %copy-start.6 = (f32[512]{0:T(512)S(1)}, f32[512]{0:T(512)}, u32[]{:S(2)}) copy-start(f32[512]{0:T(512)} %copy-done.5) | copy-start | bytes 6148
  1054.2 24.3 %copy-start.10 = (f32[512]{0:T(512)S(1)}, f32[512]{0:T(512)}, u32[]{:S(2)}) copy-start(f32[512]{0:T(512)} %copy-done.9) | copy-start | bytes 6148
  1078.5 38.0 %copy-start.8 = (f32[512]{0:T(512)S(1)}, f32[512]{0:T(512)}, u32[]{:S(2)}) copy-start(f32[512]{0:T(512)} %copy-done.7) | copy-start | bytes 6148
  1122.4 3.3 copy-start.2
Sparse Core Ops, SparseCore 0:
  19.9 158.0 all-gather.15
  179.8 155.1 all-gather.17
  504.3 48.3 all-gather.31
  554.3 48.3 all-gather.33
  604.9 155.2 all-gather.27
  762.4 155.1 all-gather.29
  919.1 18.0 all-gather.23
  939.3 19.1 all-gather.21
  960.0 49.2 all-gather.25
  1019.1 48.0 all-gather.19

commit v2 on v1

--- a/solution.py
+++ b/solution.py
@@ -14,6 +14,7 @@
 VMEM_LIMIT = 67_000_000
 BF16 = jnp.bfloat16
 F32 = jnp.float32
+MESH = pl.DeviceIdType.MESH
 
 
 def norm_f32(hid_f32, weight_f32):
@@ -23,54 +24,154 @@
     return centered * lax.rsqrt(var_val + LN_EPS) * weight_f32
 
 
-def rope_tables(positions):
-    inv_freq = ROPE_BASE ** (-jnp.arange(0, HEAD_DIM, 2, dtype=F32) / HEAD_DIM)
-    angles = positions.astype(F32)[:, None] * inv_freq[None, :]
-    cos_t = jnp.repeat(jnp.cos(angles), 2, axis=1)
-    sin_t = jnp.repeat(jnp.sin(angles), 2, axis=1)
-    sign = jnp.where(jnp.arange(HEAD_DIM) % 2 == 0, -1.0, 1.0).astype(F32)
-    return cos_t, sin_t * sign[None, :]
-
-
 def rotate(x, cos_t, sin_t):
     lane = lax.broadcasted_iota(jnp.int32, x.shape, 1)
     swapped = jnp.where(lane % 2 == 0, pltpu.roll(x, HEAD_DIM - 1, 1), pltpu.roll(x, 1, 1))
     return x * cos_t + swapped * sin_t
 
 
-def qkv_kernel(dev_ref, h_ref, wq_ref, wk_ref, wv_ref, cos_ref, sin_ref, q_ref, k_ref, kt_ref, v_ref, vt_ref):
-    h = h_ref[...]
-    cos_t, sin_t = cos_ref[...], sin_ref[...]
-    for n in range(q_ref.shape[1] // HEAD_DIM):
-        cols = slice(n * HEAD_DIM, (n + 1) * HEAD_DIM)
-        q_ref[:, cols] = rotate(jnp.dot(h, wq_ref[:, cols], preferred_element_type=F32), cos_t, sin_t).astype(BF16)
-    k = rotate(jnp.dot(h, wk_ref[...], preferred_element_type=F32), cos_t, sin_t)
-    k_ref[...] = k.astype(BF16)
-    kt_ref[...] = k.T.astype(BF16)
-    v = jnp.dot(h, wv_ref[...], preferred_element_type=F32)
-    v_ref[...] = v.astype(BF16)
-    vt_ref[...] = v.T.astype(BF16)
-
-
-def qkv_proj(dev, h_all, w_q, w_k, w_v, cos_t, sin_t, width, bm=512):
-    seq, feat = h_all.shape
-    rows = lambda i, d: (i, 0)
-    cols = lambda i, d: (0, i)
-    mine = lambda i, d: (0, d[0])
-    return pl.pallas_call(
-        qkv_kernel,
-        grid_spec=pltpu.PrefetchScalarGridSpec(
-            num_scalar_prefetch=1, grid=(seq // bm,),
-            in_specs=[pl.BlockSpec((bm, feat), rows), pl.BlockSpec((feat, width), mine), pl.BlockSpec((feat, HEAD_DIM), mine),
-                      pl.BlockSpec((feat, HEAD_DIM), mine), pl.BlockSpec((bm, HEAD_DIM), rows), pl.BlockSpec((bm, HEAD_DIM), rows)],
-            out_specs=[pl.BlockSpec((bm, width), rows), pl.BlockSpec((bm, HEAD_DIM), rows), pl.BlockSpec((HEAD_DIM, bm), cols),
-                       pl.BlockSpec((bm, HEAD_DIM), rows), pl.BlockSpec((HEAD_DIM, bm), cols)]),
-        out_shape=[jax.ShapeDtypeStruct((seq, width), BF16), jax.ShapeDtypeStruct((seq, HEAD_DIM), BF16),
-                   jax.ShapeDtypeStruct((HEAD_DIM, seq), BF16), jax.ShapeDtypeStruct((seq, HEAD_DIM), BF16),
-                   jax.ShapeDtypeStruct((HEAD_DIM, seq), BF16)],
-        compiler_params=pltpu.CompilerParams(vmem_limit_bytes=VMEM_LIMIT),
-        cost_estimate=pl.CostEstimate(flops=2 * seq * feat * (width + 256), bytes_accessed=seq * feat * 2, transcendentals=0),
-        name="qkv_proj")(dev, h_all, w_q, w_k, w_v, cos_t, sin_t)
+def flip(i, bit):
+    return i + bit - 2 * bit * ((i // bit) % 2)
+
+X, Y, Z = 2, 4, 1
+
+def gather_qkv_kernel(h_ref, pos_ref, freq_ref, wq_ref, wk_ref, wv_ref, hall_ref, q_ref, k_ref, kt_ref, v_ref, vt_ref, cos_ref, sin_ref,
+                      w_scr, buf, pos_all, pos_send, pos_recv, send, recv, w_sem, load_sem, store_sem):
+    me = lax.axis_index("sp")
+    rows = h_ref.shape[0]
+    half = rows // 2
+    width = q_ref.shape[1]
+    peers = [flip(me, 1), flip(me, 2), flip(flip(me, 2), 1), flip(me, 4), flip(flip(me, 4), 1), flip(flip(me, 4), 2), flip(flip(flip(me, 4), 2), 1)]
+    barrier = pltpu.get_barrier_semaphore()
+    for p in peers:
+        pl.semaphore_signal(barrier, inc=1, device_id={"sp": p}, device_id_type=MESH)
+    pl.semaphore_wait(barrier, len(peers))
+
+    def piece(owner, part):
+        return pl.ds(pl.multiple_of(owner * rows + part * half, half), half)
+
+    def remote(n, src, owner, part, to):
+        return pltpu.make_async_remote_copy(src_ref=src, dst_ref=hall_ref.at[piece(owner, part)], send_sem=send.at[n], recv_sem=recv.at[n],
+                                            device_id={"sp": to}, device_id_type=MESH)
+    xn, yn, zn = flip(me, X), flip(me, Y), flip(me, Z)
+    dn = flip(xn, Y)
+    own = lambda part: h_ref.at[pl.ds(part * half, half)]
+    got = lambda owner, part: hall_ref.at[piece(owner, part)]
+    pos_copies = [pltpu.make_async_remote_copy(src_ref=pos_ref, dst_ref=pos_all.at[me], send_sem=pos_send.at[i], recv_sem=pos_recv.at[i],
+                                               device_id={"sp": p}, device_id_type=MESH) for i, p in enumerate(peers)]
+    for c in pos_copies:
+        c.start()
+    s = [remote(0, own(0), me, 0, xn), remote(1, own(1), me, 1, yn), remote(2, own(1), me, 1, xn), remote(3, own(0), me, 0, yn),
+         remote(4, got(xn, 0), xn, 0, yn), remote(5, got(yn, 1), yn, 1, xn),
+         remote(6, own(0), me, 0, zn), remote(7, own(1), me, 1, zn),
+         remote(8, got(xn, 0), xn, 0, zn), remote(9, got(yn, 1), yn, 1, zn),
+         remote(10, got(xn, 1), xn, 1, zn), remote(11, got(yn, 0), yn, 0, zn),
+         remote(12, got(dn, 0), dn, 0, zn), remote(13, got(dn, 1), dn, 1, zn)]
+    for n in (0, 1, 6, 7, 2, 3):
+        s[n].start()
+    col = lambda n: pl.ds(pl.multiple_of(me * n, n), n)
+    w_copies = [pltpu.make_async_copy(wq_ref.at[:, col(width)], w_scr.at[:, pl.ds(0, width)], w_sem.at[0]),
+                pltpu.make_async_copy(wk_ref.at[:, col(HEAD_DIM)], w_scr.at[:, pl.ds(width, HEAD_DIM)], w_sem.at[1]),
+                pltpu.make_async_copy(wv_ref.at[:, col(HEAD_DIM)], w_scr.at[:, pl.ds(width + HEAD_DIM, HEAD_DIM)], w_sem.at[2])]
+    for c in w_copies:
+        c.start()
+    loads = [pltpu.make_async_copy(own(i), buf.at[i], load_sem.at[i]) for i in range(2)]
+    for c in loads:
+        c.start()
+    pos_all[me] = pos_ref[...]
+    for c in pos_copies:
+        c.wait_recv()
+
+    def compute(slot, owner, part):
+        r0 = pl.multiple_of(owner * rows + part * half, half)
+        out = pl.ds(r0, half)
+        for t in range(half // 128):
+            p = pos_all[owner, pl.ds(part * (half // 128) + t, 1), :]
+            angle = jnp.broadcast_to(p, (128, 128)).T * freq_ref[...]
+            sign = jnp.where(lax.broadcasted_iota(jnp.int32, (128, 128), 1) % 2 == 0, -1.0, 1.0)
+            tr = pl.ds(pl.multiple_of(r0 + t * 128, 128), 128)
+            cos_ref[tr, :] = jnp.cos(angle)
+            sin_ref[tr, :] = jnp.sin(angle) * sign
+        cos_t, sin_t = cos_ref[out, :], sin_ref[out, :]
+        h = buf[slot]
+        for n in range(width // 256):
+            y = jnp.dot(h, w_scr[:, n * 256:(n + 1) * 256], preferred_element_type=F32)
+            for e in range(2):
+                q_ref[out, n * 256 + e * 128: n * 256 + (e + 1) * 128] = rotate(y[:, e * 128:(e + 1) * 128], cos_t, sin_t).astype(BF16)
+        y = jnp.dot(h, w_scr[:, width:width + 256], preferred_element_type=F32)
+        k, v = rotate(y[:, :128], cos_t, sin_t), y[:, 128:]
+        k_ref[out, :] = k.astype(BF16)
+        kt_ref[:, out] = k.T.astype(BF16)
+        v_ref[out, :] = v.astype(BF16)
+        vt_ref[:, out] = v.T.astype(BF16)
+
+    def run(pairs_, slot0):
+        cps = [pltpu.make_async_copy(got(o, p), buf.at[slot0 + i], load_sem.at[slot0 + i]) for i, (o, p) in enumerate(pairs_)]
+        for c in cps:
+            c.start()
+        for c in cps:
+            c.wait()
+        (o0, p0), (o1, p1) = pairs_
+        def body(i, _):
+            compute(slot0 + i, o0 + i * (o1 - o0), p0 + i * (p1 - p0))
+            return 0
+        lax.fori_loop(0, 2, body, 0)
+
+    for c in loads:
+        c.wait()
+    stores = [pltpu.make_async_copy(buf.at[i], got(me, i), store_sem.at[i]) for i in range(2)]
+    for c in stores:
+        c.start()
+    for c in w_copies:
+        c.wait()
+    def body(i, _):
+        compute(i, me, i)
+        return 0
+    lax.fori_loop(0, 2, body, 0)
+    s[6].wait_recv(); s[7].wait_recv()
+    run([(zn, 0), (zn, 1)], 2)
+    for c in stores:
+        c.wait()
+    zx, zy, zd = flip(zn, X), flip(zn, Y), flip(dn, Z)
+    s[0].wait_recv(); s[4].start(); s[8].start()
+    s[1].wait_recv(); s[5].start(); s[9].start()
+    run([(xn, 0), (yn, 1)], 0)
+    s[8].wait_recv(); s[9].wait_recv()
+    run([(zx, 0), (zy, 1)], 2)
+    s[2].wait_recv(); s[10].start()
+    s[3].wait_recv(); s[11].start()
+    run([(xn, 1), (yn, 0)], 0)
+    s[10].wait_recv(); s[11].wait_recv()
+    run([(zx, 1), (zy, 0)], 2)
+    s[4].wait_recv(); s[12].start()
+    s[5].wait_recv(); s[13].start()
+    run([(dn, 0), (dn, 1)], 0)
+    s[12].wait_recv(); s[13].wait_recv()
+    run([(zd, 0), (zd, 1)], 2)
+    for c in s:
+        c.wait_send()
+    for c in pos_copies:
+        c.wait_send()
+
+def gather_qkv(h, pos, w_q, w_k, w_v, sp_size, cid=1):
+    rows, feat = h.shape
+    seq = rows * sp_size
+    width = w_q.shape[1] // sp_size
+    inv_freq = ROPE_BASE ** (-jnp.arange(0, HEAD_DIM, 2, dtype=F32) / HEAD_DIM)
+    freq = jnp.repeat(inv_freq, 2)[None, :]
+    any_ = pl.BlockSpec(memory_space=pl.ANY)
+    vm = pl.BlockSpec(memory_space=pltpu.VMEM)
+    return pl.pallas_call(gather_qkv_kernel,
+        in_specs=[any_, vm, vm, any_, any_, any_],
+        out_specs=[any_] + [vm] * 7,
+        out_shape=[jax.ShapeDtypeStruct((seq, feat), BF16), jax.ShapeDtypeStruct((seq, width), BF16), jax.ShapeDtypeStruct((seq, HEAD_DIM), BF16),
+                   jax.ShapeDtypeStruct((HEAD_DIM, seq), BF16), jax.ShapeDtypeStruct((seq, HEAD_DIM), BF16), jax.ShapeDtypeStruct((HEAD_DIM, seq), BF16),
+                   jax.ShapeDtypeStruct((seq, HEAD_DIM), F32), jax.ShapeDtypeStruct((seq, HEAD_DIM), F32)],
+        scratch_shapes=[pltpu.VMEM((feat, width + 256), BF16), pltpu.VMEM((4, rows // 2, feat), BF16), pltpu.VMEM((sp_size, rows // 128, 128), F32),
+                        pltpu.SemaphoreType.DMA((7,)), pltpu.SemaphoreType.DMA((7,)), pltpu.SemaphoreType.DMA((14,)), pltpu.SemaphoreType.DMA((14,)),
+                        pltpu.SemaphoreType.DMA((3,)), pltpu.SemaphoreType.DMA((4,)), pltpu.SemaphoreType.DMA((2,))],
+        compiler_params=pltpu.CompilerParams(collective_id=cid, has_side_effects=True, vmem_limit_bytes=VMEM_LIMIT),
+        name="gather_qkv")(h, pos.astype(F32).reshape(rows // 128, 128), freq, w_q, w_k, w_v)
 
 
 def do_kernel(dev_ref, g_ref, wo_ref, do_ref):
@@ -249,15 +350,14 @@
         kv_width = w_k.shape[1] // sp_size
         normed32, norm_vjp = jax.vjp(norm_f32, hidden.astype(F32), ln_weight.astype(F32))
         normed = normed32.astype(BF16)
-        pos_all = lax.all_gather(positions, 'sp', axis=0, tiled=True)
-        h_all = lax.all_gather(normed, 'sp', axis=0, tiled=True)
+        h_all, q, k, kt, v, vt, cos_t, sin_t = gather_qkv(normed, positions, w_q, w_k, w_v, sp_size)
+        d_attn, k = lax.optimization_barrier((d_attn, k))
         g_all = lax.all_gather(d_attn, 'sp', axis=0, tiled=True)
-        cos_t, sin_t = rope_tables(pos_all)
-        q, k, kt, v, vt = qkv_proj(dev1, h_all, w_q, w_k, w_v, cos_t, sin_t, width)
         o, lse = attn_forward(q, kt, v)
         o_all = lax.all_gather(o, 'sp', axis=0)
         do = do_proj(dev1, g_all, w_o, width)
         gq, gk, gv = attn_backward(q, do, lse, k, kt, vt, cos_t, sin_t)
+        gq, gk, gv, o_all = lax.optimization_barrier((gq, gk, gv, o_all))
         gq_all = lax.all_gather(gq, 'sp', axis=0)
         gk_all = lax.all_gather(gk, 'sp', axis=0)
         gv_all = lax.all_gather(gv, 'sp', axis=0)

time: 1230 us -> 1110 us (0.902)
  waiting for transfers between devices: 391 us -> 175 us
  Pallas kernels: 308 us -> 409 us
  local copies, waits for them, and re-layouts: 158 us -> 175 us
  blocking collectives: 35.8 us -> 22.3 us
    all_gather x1 -> x0, waiting for transfers between devices: 124 us -> none  [local_step(): h_all = lax.all_gather(normed, 'sp', axis=0, tiled=True)]
    pallas_call x1, Pallas kernels: 60 us -> 160 us  [gather_qkv(): pl.pallas_call(gather_qkv_kernel, in_specs=[any_, vm, vm, any_, any_, any...]
    all_gather x1, waiting for transfers between devices: 77.5 us -> 0.02 us  [local_step(): gq_all = lax.all_gather(gq, 'sp', axis=0)]
    all_gather x1, waiting for transfers between devices: 73.4 us -> 0.01 us  [local_step(): o_all = lax.all_gather(o, 'sp', axis=0)]
    all_gather x1, waiting for transfers between devices: 17.7 us -> 75.9 us  [local_step(): g_all = lax.all_gather(d_attn, 'sp', axis=0, tiled=True)]
    optimization_barrier x0 -> x1, local copies, waits for them, and re-layouts: none -> 40.8 us  [local_step(): gq, gk, gv, o_all = lax.optimization_barrier((gq, gk, gv, o_all))]
    all_gather x1 -> x0, blocking collectives: 13.6 us -> none  [local_step(): pos_all = lax.all_gather(positions, 'sp', axis=0, tiled=True)]
    unnamed x36 -> x29, local copies, waits for them, and re-layouts: 90.1 us -> 82 us
  transfers between devices with their start and end apart: 10 -> 9, of which waited for: 6 -> 3; matrix products, arithmetic and copies ran while one was open for 32% -> 37% of each run, Pallas kernels for 11% -> 23%
where the time goes in v2:
time: 1110 us; the launch traced here: 1100 us
  Pallas kernels  409 us (37%)
  matrix products  278 us (25%)
  local copies, waits for them, and re-layouts  175 us (16%)
  waiting for transfers between devices  175 us (16%)
  other arithmetic  28.5 us (3%)
  blocking collectives  22.3 us (2%)
  between operations  14.2 us (1%)
    pallas_call x1, Pallas kernels, gather_qkv(): pl.pallas_call(gather_qkv_kernel, in_specs=[any_, vm, vm, any_, any_, any...  160 us
    pallas_call x1, Pallas kernels, attn_backward(): pl.pallas_call(functools.partial(bwd_kernel, bq, bk), grid=(seq // bq,),...  146 us
    unnamed x29, local copies, waits for them, and re-layouts  82 us
    dot_general x1, matrix products, local_step(): jnp.einsum('ste,td->sed', half(o_all), g_all, preferred_element_type=F32)  79.7 us
    pallas_call x1, Pallas kernels, attn_forward(): pl.pallas_call(functools.partial(fwd_kernel, bq, bk), grid=(seq // bq,),...  79.3 us
    dot_general x1, matrix products, grad_in(): jnp.einsum('td,ste->dse', h_all, x, preferred_element_type=F32).astype(BF16)  79 us
    all_gather x1, waiting for transfers between devices, local_step(): g_all = lax.all_gather(d_attn, 'sp', axis=0, tiled=True)  75.9 us
    all_gather x1, waiting for transfers between devices, local_step(): gv_all = lax.all_gather(gv, 'sp', axis=0)  50.6 us
  transfers between devices with their start and end apart: 9, of which 3 were waited for; matrix products, arithmetic and copies ran while one was open for 37% of the time, Pallas kernels for 23%

profile of v2, /device:TPU:0, one launch (start us, length us, event | category | flops | bytes accessed | tf_op | source)
XLA Modules:
  0.0 1102.2 jit_solution(14089433638285134387)
XLA Ops:
  22.5 160.5 %gather_qkv.1 = (bf16[4096,4096]{1,0:T(8,128)(2,1)}, bf16[4096,512]{1,0:T(8,128)(2,1)}, bf16[4096,128]{1,0:T(8,128)(2,1)}, bf16[128,4096]{1,0:T(8,128)(2,1)}, bf...) custom-call(bf16[512,4096]{1,0:T(8,128)(2,1)} %fusion.22.h_ref, ...), custom_call_target="tpu_custom_call" | custom-call | tf_op jit(solution)/shard_map/gather_qkv/pallas_call | solution.py:164
  183.1 79.3 %attn_fwd.1 = (bf16[4096,512]{1,0:T(8,128)(2,1)}, f32[4,4096,1]{2,1,0:T(8,128)}) custom-call(bf16[4096,512]{1,0:T(8,128)(2,1)} %get-tuple-element.26.q_ref, bf16[128,4096]{1,0:T(8,128)(2,1)} %get-tuple-element.29.kt_ref, bf16[4096,128]{1,0:T(8,128)(2,1)} %get-tuple-element.30.v_ref), custom_call_target="tpu_custom_call" | custom-call | flops 68719476736 | bytes 16777216 | tf_op jit(solution)/shard_map/attn_fwd/pallas_call | solution.py:250
  262.5 75.9 %all-gather.14.cloned.1.call-done.g_ref = bf16[4096,4096]{1,0:T(8,128)(2,1)} async-done(((bf16[512,4096]{1,0:T(8,128)(2,1)}), bf16[4096,4096]{1,0:T(8,128)(2,1)}) %all-gather.14.cloned.1.call-update) | async-done | bytes 33554448 | tf_op jit(solution)/shard_map/all_gather | solution.py:355
  338.4 23.7 %do_proj.1.do_ref = bf16[4096,512]{1,0:T(8,128)(2,1)} custom-call(s32[1]{0:T(128)} %bitcast.1.dev_ref, bf16[4096,4096]{1,0:T(8,128)(2,1)} %all-gather.14.cloned.1.call-done.g_ref, bf16[4096,4096]{1,0:T(8,128)(2,1)} %wo_ref.1), custom_call_target="tpu_custom_call" | custom-call | flops 17179869184 | bytes 33554432 | tf_op jit(solution)/shard_map/do_proj/pallas_call | solution.py:183
  362.1 145.5 %attn_bwd.1 = (bf16[4096,512]{1,0:T(8,128)(2,1)}, bf16[4096,128]{1,0:T(8,128)(2,1)}, bf16[4096,128]{1,0:T(8,128)(2,1)}) custom-call(bf16[4096,512]{1,0:T(8,128)(2,1)} %get-tuple-element.26.q_ref, bf16[4096,512]{1,0:T(8,128)(2,1)} %do_proj.1.do_ref, f32[4,4096,1]{2,1,0:T(8,128)} %get-tuple-element.31.lse_ref, bf16[4096,128]{1,0:T(8,128)(2,1)} %get-tuple-element.32.k_ref, ...), custom_call_target="tpu_custom_call" | custom-call | flops 137438953472 | bytes 16777216 | tf_op jit(solution)/shard_map/attn_bwd/pallas_call | solution.py:322
  508.9 47.3 %all-gather.28.cloned.1.call-done = bf16[32768,128]{1,0:T(8,128)(2,1)} async-done(((bf16[4096,128]{1,0:T(8,128)(2,1)}), bf16[32768,128]{1,0:T(8,128)(2,1)}) %all-gather.28.cloned.1.call-update) | async-done | bytes 8388624 | tf_op jit(solution)/shard_map/all_gather | solution.py:362
  556.1 50.6 %all-gather.30.cloned.1.call-done = bf16[32768,128]{1,0:T(8,128)(2,1)} async-done(((bf16[4096,128]{1,0:T(8,128)(2,1)}), bf16[32768,128]{1,0:T(8,128)(2,1)}) %all-gather.30.cloned.1.call-update) | async-done | bytes 8388624 | tf_op jit(solution)/shard_map/all_gather | solution.py:363
  606.7 7.5 constant_dynamic-slice_fusion
  620.5 22.6 %fusion.33 = f32[4096,512]{0,1:S(1)} fusion(bf16[4096,512]{0,1:T(8,128)(2,1)} %bitcast.62, bf16[4096,4096]{1,0:T(8,128)(2,1)} %get-tuple-element.44), kind=kOutput, calls=%fused_computation.43 | convolution fusion | flops 17179869184 | bytes 46137344
  645.8 6.5 copy.31
  652.3 40.8 %copy.22 = bf16[8,4096,512]{1,2,0:T(8,128)(2,1)} copy(bf16[8,4096,512]{2,1,0:T(8,128)(2,1)} %bitcast.55) | data formatting | bytes 67108864 | tf_op jit(solution)/shard_map/optimization_barrier | solution.py:360
  699.5 22.6 %fusion.32 = f32[4096,512]{0,1:S(1)} fusion(bf16[4096,512]{0,1:T(8,128)(2,1)} %bitcast.63, bf16[4096,4096]{1,0:T(8,128)(2,1)} %get-tuple-element.44), kind=kOutput, calls=%fused_computation.42 | convolution fusion | flops 17179869184 | bytes 46137344
  731.2 79.7 %fusion.11 = bf16[4,512,4096]{2,1,0:T(8,128)(2,1)} fusion(bf16[4096,4096]{1,0:T(8,128)(2,1)} %all-gather.14.cloned.1.call-done.g_ref, bf16[8,4096,512]{1,2,0:T(8,128)(2,1)} %copy.22, s32[]{:T(128)S(6)} %select_n.5), kind=kOutput, calls=%fused_computation.8 | convolution fusion | flops 68727865344 | bytes 67108864 | tf_op jit(solution)/shard_map/ste,td->sed/dot_general | solution.py:374
  811.0 79.0 %fusion.6 = bf16[4096,4,512]{0,2,1:T(8,128)(2,1)} fusion(bf16[8,4096,512]{2,1,0:T(8,128)(2,1)} %bitcast.72, s32[]{:T(128)S(6)} %select_n.5, bf16[4096,4096]{1,0:T(8,128)(2,1)} %get-tuple-element.44), kind=kOutput, calls=%fused_computation.7 | convolution fusion | flops 68727865344 | bytes 67108864 | tf_op jit(solution)/shard_map/td,ste->dse/dot_general | solution.py:379
  890.0 22.6 %copy.27 = bf16[4096,2048]{1,0:T(8,128)(2,1)} copy(bf16[4096,2048]{0,1:T(8,128)(2,1)} %bitcast.59) | data formatting | bytes 33554432 | tf_op jit(solution)/shard_map/reshape | solution.py:380
  915.1 23.5 %convolution_convert_fusion = bf16[512,4096]{1,0:T(8,128)(2,1)} fusion(bf16[512,4096]{0,1:T(8,128)(2,1)S(1)} %bitcast.64, bf16[4096,4096]{1,0:T(8,128)(2,1)} %wo_ref.1), kind=kOutput, calls=%fused_computation.23 | convolution fusion | flops 17181966336 | bytes 41943040 | tf_op jit(solution)/shard_map/dot_general | solution.py:373
  941.3 10.3 fusion.31
  962.6 24.3 %fusion.30 = f32[512,4096]{1,0:T(8,128)} fusion(bf16[512,4096]{0,1:T(8,128)(2,1)} %bitcast.65, bf16[4096,4096]{1,0:T(8,128)(2,1)} %wq_ref.1), kind=kOutput, calls=%fused_computation.40 | convolution fusion | flops 17179869184 | bytes 46137344 | tf_op jit(solution)/shard_map/te,de->td/dot_general | solution.py:383
  986.9 15.7 %fusion.23 = (f32[4096]{0:T(1024)S(1)}, f32[512]{0:T(512)S(1)}, f32[512,4096]{1,0:T(8,128)}) fusion(bf16[512,4096]{1,0:T(8,128)(2,1)S(1)} %copy-done, f32[512]{0:T(512)S(1)} %copy-done.8, f32[512]{0:T(512)S(1)} %copy-done.4, f32[4096]{0:T(1024)S(1)} %copy-done.2, bf16[512,1024]{0,1:T(8,128)(2,1)S(1)} %bitcast.70, bf16[4096,1024]{1,0:T(8,128)(2,1)} %wv_ref.1, ...), kind=kOutput, calls=%fused_computation.18 | convolution fusion | flops 4315934208 | bytes 38836224 | tf_op jit(solution)/shard_map/te,de->td/dot_general | solution.py:385
  1002.6 22.3 %psum.7 = bf16[4096]{0:T(1024)(128)(2,1)} all-reduce(f32[4096]{0:T(1024)S(1)} %get-tuple-element.45), channel_id=1, replica_groups=mesh['dp'=1,'sp'=8] {'sp'}, use_global_device_ids=true, to_apply=%region_5.0 | all-reduce | flops 4096 | bytes 24576 | tf_op jit(solution)/shard_map/psum | solution.py:387
  1034.1 22.9 %copy.43 = bf16[4096,4096]{1,0:T(8,128)(2,1)} copy(bf16[4096,4096]{1,0:T(8,128)(2,1)} %all-gather.16.cloned.1.call-done) | data formatting | bytes 67108864
  1057.0 7.8 copy.44
  1064.8 7.8 copy.45
  1072.6 22.9 %copy.46 = bf16[4096,4096]{1,0:T(8,128)(2,1)} copy(bf16[4096,4096]{1,0:T(8,128)(2,1)} %all-gather.22.cloned.1.call-done) | data formatting | bytes 67108864
  (69 shorter events, 66.6 us)
Async XLA Ops:
  7.2 8.1 copy-start.9
  7.2 331.2 %all-gather.14.cloned.1.call-start = ((), (), s32[]{:S(2)}) async-start(), calls=%async_computation | async-start | bytes 37748736 | tf_op jit(solution)/shard_map/all_gather | solution.py:355
  11.3 4.7 copy-start.3
  14.7 0.5 copy-start.5
  15.3 0.7 copy-start.7
  15.3 0.7 copy-start.1
  183.0 324.6 %all-gather.24.cloned.1.call-start = ((), (), s32[]{:S(2)}) async-start(), calls=%async_computation.5 | async-start | bytes 37748736 | tf_op jit(solution)/shard_map/all_gather | solution.py:357
  262.4 293.7 %all-gather.28.cloned.1.call-start = ((), (), s32[]{:S(2)}) async-start(), calls=%async_computation.7 | async-start | bytes 9437184 | tf_op jit(solution)/shard_map/all_gather | solution.py:362
  507.6 99.1 %all-gather.30.cloned.1.call-start = ((), (), s32[]{:S(2)}) async-start(), calls=%async_computation.8 | async-start | bytes 9437184 | tf_op jit(solution)/shard_map/all_gather | solution.py:363
  508.2 302.7 %all-gather.26.cloned.1.call-start = ((), (), s32[]{:S(2)}) async-start(), calls=%async_computation.6 | async-start | bytes 37748736 | tf_op jit(solution)/shard_map/all_gather | solution.py:361
  508.8 442.9 %all-gather.20.cloned.1.call-start = ((), (), s32[]{:S(2)}) async-start(), calls=%async_computation.3 | async-start | bytes 12582912 | tf_op jit(solution)/shard_map/all_gather | solution.py:380
  652.3 299.4 %all-gather.18.cloned.1.call-start = ((), (), s32[]{:S(2)}) async-start(), calls=%async_computation.2 | async-start | bytes 12582912 | tf_op jit(solution)/shard_map/all_gather | solution.py:380
  731.2 220.5 %all-gather.22.cloned.1.call-start = ((), (), s32[]{:S(2)}) async-start(), calls=%async_computation.4 | async-start | bytes 50331648 | tf_op jit(solution)/shard_map/all_gather | solution.py:375
  810.9 223.2 %all-gather.16.cloned.1.call-start = ((), (), s32[]{:S(2)}) async-start(), calls=%async_computation.1 | async-start | bytes 50331648 | tf_op jit(solution)/shard_map/all_gather | solution.py:380
  962.6 24.3 %copy-start = (bf16[512,4096]{1,0:T(8,128)(2,1)S(1)}, bf16[512,4096]{1,0:T(8,128)(2,1)}, u32[]{:S(2)}) copy-start(bf16[512,4096]{1,0:T(8,128)(2,1)} %param.8) | copy-start | bytes 12582916
  962.6 24.3 %copy-start.2 = (f32[4096]{0:T(1024)S(1)}, f32[4096]{0:T(1024)}, u32[]{:S(2)}) copy-start(f32[4096]{0:T(1024)} %copy-done.1) | copy-start | bytes 49156
  962.6 24.3 %copy-start.4 = (f32[512]{0:T(512)S(1)}, f32[512]{0:T(512)}, u32[]{:S(2)}) copy-start(f32[512]{0:T(512)} %copy-done.3) | copy-start | bytes 6148
  962.6 24.3 %copy-start.8 = (f32[512]{0:T(512)S(1)}, f32[512]{0:T(512)}, u32[]{:S(2)}) copy-start(f32[512]{0:T(512)} %copy-done.7) | copy-start | bytes 6148
  986.9 38.0 %copy-start.6 = (f32[512]{0:T(512)S(1)}, f32[512]{0:T(512)}, u32[]{:S(2)}) copy-start(f32[512]{0:T(512)} %copy-done.5) | copy-start | bytes 6148
Sparse Core Ops, SparseCore 0:
  183.1 155.2 all-gather.13
  340.8 155.1 all-gather.23
  507.8 48.3 all-gather.27
  558.4 48.3 all-gather.29
  609.0 155.2 all-gather.25
  765.6 18.0 all-gather.19
  785.7 19.1 all-gather.17
  811.0 48.0 all-gather.21
  912.7 48.0 all-gather.15

commit v3 on v2

--- a/solution.py
+++ b/solution.py
@@ -35,8 +35,8 @@
 
 X, Y, Z = 2, 4, 1
 
-def gather_qkv_kernel(h_ref, pos_ref, freq_ref, wq_ref, wk_ref, wv_ref, hall_ref, q_ref, k_ref, kt_ref, v_ref, vt_ref, cos_ref, sin_ref,
-                      w_scr, buf, pos_all, pos_send, pos_recv, send, recv, w_sem, load_sem, store_sem):
+def gather_qkv_kernel(h_ref, pos_ref, freq_ref, wq_ref, wk_ref, wv_ref, hall_ref, ht_ref, q_ref, k_ref, kt_ref, v_ref, vt_ref, cos_ref, sin_ref,
+                      w_scr, buf, tbuf, pos_all, pos_send, pos_recv, send, recv, w_sem, load_sem, store_sem, t_sem):
     me = lax.axis_index("sp")
     rows = h_ref.shape[0]
     half = rows // 2
@@ -82,7 +82,10 @@
     for c in pos_copies:
         c.wait_recv()
 
-    def compute(slot, owner, part):
+    def t_copy(tslot, r0):
+        return pltpu.make_async_copy(tbuf.at[tslot], ht_ref.at[:, pl.ds(r0, half)], t_sem.at[tslot])
+
+    def compute(slot, owner, part, first=False):
         r0 = pl.multiple_of(owner * rows + part * half, half)
         out = pl.ds(r0, half)
         for t in range(half // 128):
@@ -94,6 +97,11 @@
             sin_ref[tr, :] = jnp.sin(angle) * sign
         cos_t, sin_t = cos_ref[out, :], sin_ref[out, :]
         h = buf[slot]
+        tslot = slot % 2
+        if first is None or not first:
+            t_copy(tslot, 0).wait()
+        tbuf[tslot] = h.T
+        t_copy(tslot, r0).start()
         for n in range(width // 256):
             y = jnp.dot(h, w_scr[:, n * 256:(n + 1) * 256], preferred_element_type=F32)
             for e in range(2):
@@ -125,7 +133,7 @@
     for c in w_copies:
         c.wait()
     def body(i, _):
-        compute(i, me, i)
+        compute(i, me, i, True)
         return 0
     lax.fori_loop(0, 2, body, 0)
     s[6].wait_recv(); s[7].wait_recv()
@@ -148,6 +156,8 @@
     run([(dn, 0), (dn, 1)], 0)
     s[12].wait_recv(); s[13].wait_recv()
     run([(zd, 0), (zd, 1)], 2)
+    for i in range(2):
+        t_copy(i, 0).wait()
     for c in s:
         c.wait_send()
     for c in pos_copies:
@@ -163,13 +173,13 @@
     vm = pl.BlockSpec(memory_space=pltpu.VMEM)
     return pl.pallas_call(gather_qkv_kernel,
         in_specs=[any_, vm, vm, any_, any_, any_],
-        out_specs=[any_] + [vm] * 7,
-        out_shape=[jax.ShapeDtypeStruct((seq, feat), BF16), jax.ShapeDtypeStruct((seq, width), BF16), jax.ShapeDtypeStruct((seq, HEAD_DIM), BF16),
+        out_specs=[any_, any_] + [vm] * 7,
+        out_shape=[jax.ShapeDtypeStruct((seq, feat), BF16), jax.ShapeDtypeStruct((feat, seq), BF16), jax.ShapeDtypeStruct((seq, width), BF16), jax.ShapeDtypeStruct((seq, HEAD_DIM), BF16),
                    jax.ShapeDtypeStruct((HEAD_DIM, seq), BF16), jax.ShapeDtypeStruct((seq, HEAD_DIM), BF16), jax.ShapeDtypeStruct((HEAD_DIM, seq), BF16),
                    jax.ShapeDtypeStruct((seq, HEAD_DIM), F32), jax.ShapeDtypeStruct((seq, HEAD_DIM), F32)],
-        scratch_shapes=[pltpu.VMEM((feat, width + 256), BF16), pltpu.VMEM((4, rows // 2, feat), BF16), pltpu.VMEM((sp_size, rows // 128, 128), F32),
+        scratch_shapes=[pltpu.VMEM((feat, width + 256), BF16), pltpu.VMEM((4, rows // 2, feat), BF16), pltpu.VMEM((2, feat, rows // 2), BF16), pltpu.VMEM((sp_size, rows // 128, 128), F32),
                         pltpu.SemaphoreType.DMA((7,)), pltpu.SemaphoreType.DMA((7,)), pltpu.SemaphoreType.DMA((14,)), pltpu.SemaphoreType.DMA((14,)),
-                        pltpu.SemaphoreType.DMA((3,)), pltpu.SemaphoreType.DMA((4,)), pltpu.SemaphoreType.DMA((2,))],
+                        pltpu.SemaphoreType.DMA((3,)), pltpu.SemaphoreType.DMA((4,)), pltpu.SemaphoreType.DMA((2,)), pltpu.SemaphoreType.DMA((2,))],
         compiler_params=pltpu.CompilerParams(collective_id=cid, has_side_effects=True, vmem_limit_bytes=VMEM_LIMIT),
         name="gather_qkv")(h, pos.astype(F32).reshape(rows // 128, 128), freq, w_q, w_k, w_v)
 
@@ -196,17 +206,12 @@
     return jnp.concatenate([x[:, n * HEAD_DIM:(n + 1) * HEAD_DIM] for n in range(x.shape[1] // HEAD_DIM)], axis=0)
 
 
-def unstack_heads(ref, x, rows):
-    for n in range(x.shape[0] // rows):
-        ref[:, n * HEAD_DIM:(n + 1) * HEAD_DIM] = x[n * rows:(n + 1) * rows].astype(ref.dtype)
-
-
 def causal(shape, bq, offset):
     rows = lax.rem(lax.broadcasted_iota(jnp.int32, shape, 0), bq) + offset
     return rows >= lax.broadcasted_iota(jnp.int32, shape, 1)
 
 
-def fwd_kernel(bq, bk, q_ref, kt_ref, v_ref, o_ref, lse_ref, s_scr):
+def fwd_kernel(bq, bk, q_ref, kt_ref, v_ref, ot_ref, lse_ref, s_scr):
     qi = pl.program_id(0)
     q = stack_heads(q_ref[...])
     rows = q.shape[0]
@@ -240,7 +245,9 @@
 
     l, o = lax.fori_loop(0, nfull + 1, value_step, (jnp.zeros((rows, 128), F32), jnp.zeros((rows, HEAD_DIM), F32)))
     l = jnp.sum(l, axis=1, keepdims=True)
-    unstack_heads(o_ref, o / l, bq)
+    o = (o / l).astype(BF16)
+    for n in range(rows // bq):
+        ot_ref[n * HEAD_DIM:(n + 1) * HEAD_DIM, :] = o[n * bq:(n + 1) * bq].T
     lse_ref[...] = (m + jnp.log2(l)).reshape(lse_ref.shape)
 
 
@@ -251,15 +258,17 @@
         functools.partial(fwd_kernel, bq, bk), grid=(seq // bq,),
         in_specs=[pl.BlockSpec((bq, width), lambda i: (i, 0)), pl.BlockSpec((HEAD_DIM, seq), lambda i: (0, 0)),
                   pl.BlockSpec((seq, HEAD_DIM), lambda i: (0, 0))],
-        out_specs=[pl.BlockSpec((bq, width), lambda i: (i, 0)), pl.BlockSpec((heads, bq, 1), lambda i: (0, i, 0))],
-        out_shape=[jax.ShapeDtypeStruct((seq, width), BF16), jax.ShapeDtypeStruct((heads, seq, 1), F32)],
+        out_specs=[pl.BlockSpec((width, bq), lambda i: (0, i)), pl.BlockSpec((heads, bq, 1), lambda i: (0, i, 0))],
+        out_shape=[jax.ShapeDtypeStruct((width, seq), BF16), jax.ShapeDtypeStruct((heads, seq, 1), F32)],
         scratch_shapes=[pltpu.VMEM((seq // bk, heads * bq, bk), F32)],
         compiler_params=pltpu.CompilerParams(vmem_limit_bytes=VMEM_LIMIT),
         cost_estimate=pl.CostEstimate(flops=8 * seq * seq * width, bytes_accessed=seq * width * 8, transcendentals=0),
         name="attn_fwd")(q, kt, v)
 
 
-def bwd_kernel(bq, bk, q_ref, do_ref, lse_ref, k_ref, kt_ref, vt_ref, cos_ref, sin_ref, gq_ref, gk_ref, gv_ref, p_scr, dp_scr, dkt_scr, dvt_scr):
+def bwd_kernel(bq, bk, more, *refs):
+    q_ref, do_ref, lse_ref, k_ref, kt_ref, vt_ref, cos_ref, sin_ref = refs[:8]
+    gq_ref, dkt_ref, dvt_ref, p_scr, dp_scr = refs[-5:]
     qi = pl.program_id(0)
     q = stack_heads(q_ref[...])
     do = stack_heads(do_ref[...])
@@ -271,8 +280,8 @@
 
     @pl.when(qi == 0)
     def _():
-        dkt_scr[...] = jnp.zeros_like(dkt_scr)
-        dvt_scr[...] = jnp.zeros_like(dvt_scr)
+        dkt_ref[...] = refs[8][...] if more else jnp.zeros_like(dkt_ref)
+        dvt_ref[...] = refs[9][...] if more else jnp.zeros_like(dvt_ref)
 
     def prob_step(j, r, masked):
         sl = pl.ds(pl.multiple_of(j * bk, bk), bk)
@@ -286,7 +295,7 @@
             r = r + pd[:, t * 128:(t + 1) * 128]
         p_scr[j] = p
         dp_scr[j] = dp
-        dvt_scr[:, sl] += jnp.dot(do_t, p.astype(BF16), preferred_element_type=F32)
+        dvt_ref[:, sl] += jnp.dot(do_t, p.astype(BF16), preferred_element_type=F32)
         return r
 
     r = lax.fori_loop(0, nfull, lambda j, r: prob_step(j, r, False), jnp.zeros((rows, 128), F32))
@@ -296,45 +305,132 @@
     def grad_step(j, dq):
         sl = pl.ds(pl.multiple_of(j * bk, bk), bk)
         ds = (p_scr[j] * (dp_scr[j] - r) * SCALE).astype(BF16)
-        dkt_scr[:, sl] += jnp.dot(q_t, ds, preferred_element_type=F32)
+        dkt_ref[:, sl] += jnp.dot(q_t, ds, preferred_element_type=F32)
         return dq + jnp.dot(ds, k_ref[sl, :], preferred_element_type=F32)
 
     dq = lax.fori_loop(0, nfull + 1, grad_step, jnp.zeros((rows, HEAD_DIM), F32))
     dq = dq.astype(BF16).astype(F32)
-    start = pl.ds(pl.multiple_of(qi * bq, bq), bq)
-    cos_t, sin_t = cos_ref[start, :], sin_ref[start, :]
+    cos_t, sin_t = cos_ref[...], sin_ref[...]
     for n in range(rows // bq):
         gq_ref[:, n * HEAD_DIM:(n + 1) * HEAD_DIM] = rotate(dq[n * bq:(n + 1) * bq], cos_t, -sin_t).astype(BF16)
 
-    @pl.when(qi == pl.num_programs(0) - 1)
-    def _():
-        dk = dkt_scr[...].T.astype(BF16).astype(F32)
-        gk_ref[...] = rotate(dk, cos_ref[...], -sin_ref[...]).astype(BF16)
-        gv_ref[...] = dvt_scr[...].T.astype(BF16)
-
-
-def attn_backward(q, do, lse, k, kt, vt, cos_t, sin_t, bq=256, bk=512):
-    seq, width = q.shape
-    heads = width // HEAD_DIM
-    tile = pl.BlockSpec((bq, width), lambda i: (i, 0))
+
+def kv_kernel(dkt_ref, dvt_ref, cos_ref, sin_ref, gkv_ref):
+    dk = dkt_ref[...].T.astype(BF16).astype(F32)
+    gkv_ref[:, :HEAD_DIM] = rotate(dk, cos_ref[...], -sin_ref[...]).astype(BF16)
+    gkv_ref[:, HEAD_DIM:] = dvt_ref[...].T.astype(BF16)
+
+
+def attn_backward(part, q, do, lse, k, kt, vt, cos_t, sin_t, sums=None, bq=256, bk=512):
+    seq = q.shape[0]
+    width, heads = 2 * HEAD_DIM, 2
+    tile = pl.BlockSpec((bq, width), lambda i: (i, part))
+    rope = pl.BlockSpec((bq, HEAD_DIM), lambda i: (i, 0))
     tall = pl.BlockSpec((seq, HEAD_DIM), lambda i: (0, 0))
     wide = pl.BlockSpec((HEAD_DIM, seq), lambda i: (0, 0))
+    last = sums is not None
+    params = dict(compiler_params=pltpu.CompilerParams(vmem_limit_bytes=VMEM_LIMIT),
+                  cost_estimate=pl.CostEstimate(flops=8 * seq * seq * width, bytes_accessed=seq * width * 8, transcendentals=0))
     return pl.pallas_call(
-        functools.partial(bwd_kernel, bq, bk), grid=(seq // bq,),
-        in_specs=[tile, tile, pl.BlockSpec((heads, bq, 1), lambda i: (0, i, 0)), tall, wide, wide, tall, tall],
-        out_specs=[tile, tall, tall],
-        out_shape=[jax.ShapeDtypeStruct((seq, width), BF16), jax.ShapeDtypeStruct((seq, HEAD_DIM), BF16),
-                   jax.ShapeDtypeStruct((seq, HEAD_DIM), BF16)],
-        scratch_shapes=[pltpu.VMEM((seq // bk, heads * bq, bk), F32), pltpu.VMEM((seq // bk, heads * bq, bk), F32),
-                        pltpu.VMEM((HEAD_DIM, seq), F32), pltpu.VMEM((HEAD_DIM, seq), F32)],
+        functools.partial(bwd_kernel, bq, bk, last), grid=(seq // bq,),
+        in_specs=[tile, tile, pl.BlockSpec((heads, bq, 1), lambda i: (part, i, 0)), tall, wide, wide, rope, rope] + ([wide, wide] if last else []),
+        out_specs=[pl.BlockSpec((bq, width), lambda i: (i, 0)), wide, wide],
+        out_shape=[jax.ShapeDtypeStruct((seq, width), BF16), jax.ShapeDtypeStruct((HEAD_DIM, seq), F32), jax.ShapeDtypeStruct((HEAD_DIM, seq), F32)],
+        scratch_shapes=[pltpu.VMEM((seq // bk, heads * bq, bk), F32), pltpu.VMEM((seq // bk, heads * bq, bk), F32)],
+        name="attn_bwd", **params)(q, do, lse, k, kt, vt, cos_t, sin_t, *(sums or ()))
+
+
+def kv_grad(dkt, dvt, cos_t, sin_t, bq=512):
+    seq = dkt.shape[1]
+    wide = pl.BlockSpec((HEAD_DIM, bq), lambda i: (0, i))
+    rope = pl.BlockSpec((bq, HEAD_DIM), lambda i: (i, 0))
+    return pl.pallas_call(kv_kernel, grid=(seq // bq,), in_specs=[wide, wide, rope, rope],
+                          out_specs=pl.BlockSpec((bq, 2 * HEAD_DIM), lambda i: (i, 0)),
+                          out_shape=jax.ShapeDtypeStruct((seq, 2 * HEAD_DIM), BF16), name="kv_grad")(dkt, dvt, cos_t, sin_t)
+
+
+def dw_o_kernel(core_ref, ot_ref, g_ref, final_ref, send_ref):
+    y = jnp.dot(ot_ref[...], g_ref[...], preferred_element_type=F32).astype(BF16)
+    final_ref[...] = y
+    send_ref[...] = y
+
+
+def dw_o_half(core, ot_all, g_all, bn=1024):
+    n_dev, width, seq = ot_all.shape
+    feat = g_all.shape[1]
+    half = n_dev // 2
+    return pl.pallas_call(
+        dw_o_kernel,
+        grid_spec=pltpu.PrefetchScalarGridSpec(
+            num_scalar_prefetch=1, grid=(feat // bn, half),
+            in_specs=[pl.BlockSpec((None, width, seq), lambda j, s, c: (c[0] * half + s, 0, 0)), pl.BlockSpec((seq, bn), lambda j, s, c: (0, j))],
+            out_specs=[pl.BlockSpec((width, bn), lambda j, s, c: (c[0] * half + s, j)), pl.BlockSpec((width, bn), lambda j, s, c: (s, j))]),
+        out_shape=[jax.ShapeDtypeStruct((n_dev * width, feat), BF16), jax.ShapeDtypeStruct((half * width, feat), BF16)],
         compiler_params=pltpu.CompilerParams(vmem_limit_bytes=VMEM_LIMIT),
-        cost_estimate=pl.CostEstimate(flops=16 * seq * seq * width, bytes_accessed=seq * width * 8, transcendentals=0),
-        name="attn_bwd")(q, do, lse, k, kt, vt, cos_t, sin_t)
+        cost_estimate=pl.CostEstimate(flops=n_dev * width * feat * seq, bytes_accessed=seq * feat * 6, transcendentals=0),
+        name="dw_o_half")(core, ot_all, g_all)
+
+
+def dw_kernel(n_final, n_copy, core_ref, ht_ref, x_ref, *refs):
+    recv = refs[:n_copy]
+    outs = refs[-(n_final + 1 + n_copy):]
+    y = jnp.dot(ht_ref[...], x_ref[...], preferred_element_type=F32).astype(BF16)
+    w = y.shape[1] // n_final
+    for n in range(n_final):
+        outs[n][...] = y[:, n * w:(n + 1) * w]
+    outs[n_final][...] = y
+    for n in range(n_copy):
+        outs[n_final + 1 + n][...] = recv[n][...]
+
+
+def dw_half(name, core, ht, x_all, finals, final_shapes, final_cols, copies, bm=1024):
+    n_dev, seq, cols = x_all.shape
+    feat = ht.shape[0]
+    half = n_dev // 2
+    n_final = len(final_shapes)
+    w = cols // n_final
+    hbm = pl.BlockSpec(memory_space=pl.ANY)
+    ins = [ht, x_all] + [c[0] for c in copies]
+    in_specs = [pl.BlockSpec((bm, seq), lambda i, s, c: (i, 0)), pl.BlockSpec((None, seq, cols), lambda i, s, c: (c[0] * half + s, 0, 0))]
+    in_specs += [c[1] for c in copies]
+    out_specs = [pl.BlockSpec((bm, w), functools.partial(lambda f, i, s, c: (i, f(c[0] * half + s)), f)) for f in final_cols]
+    out_specs += [pl.BlockSpec((bm, cols), lambda i, s, c: (i, s))] + [c[3] for c in copies]
+    out_shape = [jax.ShapeDtypeStruct(sh, BF16) for sh in final_shapes] + [jax.ShapeDtypeStruct((feat, half * cols), BF16)]
+    out_shape += [jax.ShapeDtypeStruct(c[2].shape, BF16) for c in copies]
+    aliases = {}
+    for n, f in enumerate(finals):
+        if f is not None:
+            aliases[1 + len(ins)] = n
+            ins.append(f)
+            in_specs.append(hbm)
+    for n, c in enumerate(copies):
+        aliases[1 + len(ins)] = n_final + 1 + n
+        ins.append(c[2])
+        in_specs.append(hbm)
+    return pl.pallas_call(
+        functools.partial(dw_kernel, n_final, len(copies)),
+        grid_spec=pltpu.PrefetchScalarGridSpec(num_scalar_prefetch=1, grid=(feat // bm, half), in_specs=in_specs, out_specs=out_specs),
+        out_shape=out_shape, input_output_aliases=aliases,
+        compiler_params=pltpu.CompilerParams(vmem_limit_bytes=VMEM_LIMIT),
+        cost_estimate=pl.CostEstimate(flops=2 * seq * feat * half * cols, bytes_accessed=seq * feat * 6, transcendentals=0),
+        name=name)(core, *ins)
+
+
+def copy_kernel(core_ref, recv_ref, _, out_ref):
+    out_ref[...] = recv_ref[...]
+
+
+def copy_in(core, recv, final, grid, recv_spec, final_spec):
+    return pl.pallas_call(
+        copy_kernel,
+        grid_spec=pltpu.PrefetchScalarGridSpec(num_scalar_prefetch=1, grid=grid, in_specs=[recv_spec, pl.BlockSpec(memory_space=pl.ANY)],
+                                               out_specs=final_spec),
+        out_shape=jax.ShapeDtypeStruct(final.shape, BF16), input_output_aliases={2: 0},
+        compiler_params=pltpu.CompilerParams(vmem_limit_bytes=VMEM_LIMIT), name="copy_in")(core, recv, final)
 
 
 def solution(mesh):
     sp_size = mesh.shape['sp']
-    pairs = [[i, i + 1] for i in range(0, sp_size, 2)]
     row_spec = P(('dp', 'sp'), None)
     pos_spec = P(('dp', 'sp'))
     full_spec = P(None, None)
@@ -345,44 +441,63 @@
         core = lax.rem(dev, 2)
         dev1 = dev.reshape(1)
         local_rows, feat = hidden.shape
-        seq = local_rows * sp_size
         width = w_q.shape[1] // sp_size
-        kv_width = w_k.shape[1] // sp_size
         normed32, norm_vjp = jax.vjp(norm_f32, hidden.astype(F32), ln_weight.astype(F32))
         normed = normed32.astype(BF16)
-        h_all, q, k, kt, v, vt, cos_t, sin_t = gather_qkv(normed, positions, w_q, w_k, w_v, sp_size)
+        h_all, ht, q, k, kt, v, vt, cos_t, sin_t = gather_qkv(normed, positions, w_q, w_k, w_v, sp_size)
         d_attn, k = lax.optimization_barrier((d_attn, k))
         g_all = lax.all_gather(d_attn, 'sp', axis=0, tiled=True)
-        o, lse = attn_forward(q, kt, v)
-        o_all = lax.all_gather(o, 'sp', axis=0)
+        ot, lse = attn_forward(q, kt, v)
+        ot, g_all = lax.optimization_barrier((ot, g_all))
+        ot_all = lax.all_gather(ot, 'sp', axis=0)
         do = do_proj(dev1, g_all, w_o, width)
-        gq, gk, gv = attn_backward(q, do, lse, k, kt, vt, cos_t, sin_t)
-        gq, gk, gv, o_all = lax.optimization_barrier((gq, gk, gv, o_all))
-        gq_all = lax.all_gather(gq, 'sp', axis=0)
-        gk_all = lax.all_gather(gk, 'sp', axis=0)
-        gv_all = lax.all_gather(gv, 'sp', axis=0)
+        ga, dkt, dvt = attn_backward(0, q, do, lse, k, kt, vt, cos_t, sin_t)
+        ga, ot_all = lax.optimization_barrier((ga, ot_all))
+        ga_all = lax.all_gather(ga, 'sp', axis=0)
+        gb, dkt, dvt = attn_backward(1, q, do, lse, k, kt, vt, cos_t, sin_t, (dkt, dvt))
+        gc = kv_grad(dkt, dvt, cos_t, sin_t)
+        gc, ga_all = lax.optimization_barrier((gc, ga_all))
+        gc_all = lax.all_gather(gc, 'sp', axis=0)
+        gb, gc_all = lax.optimization_barrier((gb, gc_all))
+        gb_all = lax.all_gather(gb, 'sp', axis=0)
+        core1 = core.reshape(1)
+        swap = lambda x: lax.ppermute(x, 'sp', [(i, i ^ 1) for i in range(sp_size)])
+        n_half = sp_size // 2
+        piece = 2 * HEAD_DIM
 
         def own_rows(x_all):
             x = lax.dynamic_slice_in_dim(x_all, dev * local_rows, local_rows, axis=1)
             return jnp.transpose(x, (1, 0, 2)).reshape(local_rows, -1)
 
-        def half(x_all):
-            n = sp_size // 2
-            return lax.dynamic_slice_in_dim(x_all, core * n, n, axis=0)
-
-        attn_out = jnp.dot(own_rows(o_all), w_o, preferred_element_type=F32).astype(BF16)
-        dw_o = jnp.einsum('ste,td->sed', half(o_all), g_all, preferred_element_type=F32).astype(BF16)
-        dw_o = lax.all_gather(dw_o.reshape(-1, feat), 'sp', axis=0, tiled=True, axis_index_groups=pairs)
-
-        def grad_in(x_all):
-            x = half(x_all)
-            y = jnp.einsum('td,ste->dse', h_all, x, preferred_element_type=F32).astype(BF16)
-            return lax.all_gather(y.reshape(feat, -1), 'sp', axis=1, tiled=True, axis_index_groups=pairs)
-
-        dw_q, dw_k, dw_v = grad_in(gq_all), grad_in(gk_all), grad_in(gv_all)
-        d_normed = (jnp.einsum('te,de->td', own_rows(gq_all), w_q, preferred_element_type=F32)
-                    + jnp.einsum('te,de->td', own_rows(gk_all), w_k, preferred_element_type=F32)
-                    + jnp.einsum('te,de->td', own_rows(gv_all), w_v, preferred_element_type=F32))
+        dw_o, o_send = dw_o_half(core1, ot_all, g_all)
+        o_recv = swap(o_send)
+        ot_own = lax.dynamic_slice_in_dim(ot_all, dev * local_rows, local_rows, axis=2).reshape(feat, local_rows)
+        attn_out = jnp.einsum('et,ed->td', ot_own, w_o, preferred_element_type=F32).astype(BF16)
+        steps = (feat // 1024) * n_half
+        o_rows = feat // 2 // steps
+        ride_o = (o_recv, pl.BlockSpec((o_rows, feat), lambda i, s, c: (i * n_half + s, 0)), dw_o,
+                  pl.BlockSpec((o_rows, feat), lambda i, s, c: ((1 - c[0]) * steps + i * n_half + s, 0)))
+        dw_q, a_send, dw_o = dw_half('dw_qa', core1, ht, ga_all, [None], [w_q.shape], [lambda d: 2 * d], [ride_o])
+        a_recv = swap(a_send)
+        ride_a = (a_recv, pl.BlockSpec((1024, piece), lambda i, s, c: (i, s)), dw_q,
+                  pl.BlockSpec((1024, piece), lambda i, s, c: (i, 2 * ((1 - c[0]) * n_half + s))))
+        dw_k, dw_v, c_send, dw_q = dw_half('dw_kv', core1, ht, gc_all, [None, None], [w_k.shape, w_v.shape], [lambda d: d, lambda d: d], [ride_a])
+        c_recv = swap(c_send)
+        ride_k = (c_recv, pl.BlockSpec((1024, HEAD_DIM), lambda i, s, c: (i, 2 * s)), dw_k,
+                  pl.BlockSpec((1024, HEAD_DIM), lambda i, s, c: (i, (1 - c[0]) * n_half + s)))
+        ride_v = (c_recv, pl.BlockSpec((1024, HEAD_DIM), lambda i, s, c: (i, 2 * s + 1)), dw_v,
+                  pl.BlockSpec((1024, HEAD_DIM), lambda i, s, c: (i, (1 - c[0]) * n_half + s)))
+        dw_q, b_send, dw_k, dw_v = dw_half('dw_qb', core1, ht, gb_all, [dw_q], [w_q.shape], [lambda d: 2 * d + 1], [ride_k, ride_v])
+        b_recv = swap(b_send)
+        dw_q = copy_in(core1, b_recv, dw_q, (feat // 1024, n_half), pl.BlockSpec((1024, piece), lambda i, s, c: (i, s)),
+                       pl.BlockSpec((1024, piece), lambda i, s, c: (i, 2 * ((1 - c[0]) * n_half + s) + 1)))
+
+        gq_tok = jnp.concatenate([own_rows(ga_all).reshape(local_rows, sp_size, piece), own_rows(gb_all).reshape(local_rows, sp_size, piece)],
+                                 axis=2).reshape(local_rows, -1)
+        gkv_tok = own_rows(gc_all).reshape(local_rows, sp_size, 2, HEAD_DIM)
+        d_normed = (jnp.einsum('te,de->td', gq_tok, w_q, preferred_element_type=F32)
+                    + jnp.einsum('te,de->td', gkv_tok[:, :, 0].reshape(local_rows, -1), w_k, preferred_element_type=F32)
+                    + jnp.einsum('te,de->td', gkv_tok[:, :, 1].reshape(local_rows, -1), w_v, preferred_element_type=F32))
         d_hid, d_lnw = norm_vjp(d_normed)
         d_lnw = lax.psum(d_lnw, 'sp')
         return (attn_out, d_hid.astype(BF16), d_lnw.astype(BF16), dw_q, dw_k, dw_v, dw_o)

time: 1110 us -> 1040 us (0.937)
  Pallas kernels: 409 us -> 695 us
  matrix products: 278 us -> 74.6 us
  local copies, waits for them, and re-layouts: 175 us -> 35.3 us
    pallas_call x1 -> x8, Pallas kernels: 146 us -> 430 us  [the longest x2 170 us: attn_backward(): pl.pallas_call(functools.partial(bwd_kernel, bq, bk, last), grid=(seq //...]
    dot_general x6 -> x4, matrix products: 232 us -> 74.6 us  [the longest x1 24.5 us: local_step(): jnp.einsum('te,de->td', gq_tok, w_q, preferred_element_type=F32)]
    unnamed x29 -> x24, local copies, waits for them, and re-layouts: 82 us -> 11.1 us
    unnamed x2 -> x0, matrix products: 45.2 us -> none
    all_gather x8 -> x4, waiting for transfers between devices: 97.9 us -> 53.8 us  [the longest x1 50 us: local_step(): ot_all = lax.all_gather(ot, 'sp', axis=0)]
    optimization_barrier x1 -> x0, local copies, waits for them, and re-layouts: 40.8 us -> none  [local_step(): gq, gk, gv, o_all = lax.optimization_barrier((gq, gk, gv, o_all))]
    ppermute x0 -> x4, waiting for transfers between devices: none -> 36.3 us  [local_step(): swap = lambda x: lax.ppermute(x, 'sp', [(i, i ^ 1) for i in range(sp_size)])]
    reshape x3 -> x0, local copies, waits for them, and re-layouts: 35.5 us -> none  [grad_in(): y.reshape(feat, -1)]
  transfers between devices with their start and end apart: 9 -> 9, of which waited for: 3 -> 5; matrix products, arithmetic and copies ran while one was open for 37% -> 12% of each run, Pallas kernels for 23% -> 45%
where the time goes in v3:
time: 1040 us; the launch traced here: 1030 us
  Pallas kernels  695 us (67%)
  waiting for transfers between devices  165 us (16%)
  matrix products  74.6 us (7%)
  local copies, waits for them, and re-layouts  35.3 us (3%)
  other arithmetic  25.6 us (2%)
  blocking collectives  22.3 us (2%)
  between operations  14.2 us (1%)
    pallas_call x2, Pallas kernels, attn_backward(): pl.pallas_call(functools.partial(bwd_kernel, bq, bk, last), grid=(seq //...  170 us
    pallas_call x1, Pallas kernels, gather_qkv(): pl.pallas_call(gather_qkv_kernel, in_specs=[any_, vm, vm, any_, any_, any...  162 us
    pallas_call x3, Pallas kernels, dw_half(): pl.pallas_call(functools.partial(dw_kernel, n_final, len(copies)), grid_s...  158 us
    pallas_call x1, Pallas kernels, dw_o_half(): pl.pallas_call(dw_o_kernel, grid_spec=pltpu.PrefetchScalarGridSpec(num_sc...  81.2 us
    pallas_call x1, Pallas kernels, attn_forward(): pl.pallas_call(functools.partial(fwd_kernel, bq, bk), grid=(seq // bq,),...  80.2 us
    all_gather x1, waiting for transfers between devices, local_step(): g_all = lax.all_gather(d_attn, 'sp', axis=0, tiled=True)  75.1 us
    all_gather x1, waiting for transfers between devices, local_step(): ot_all = lax.all_gather(ot, 'sp', axis=0)  50 us
    ppermute x4, waiting for transfers between devices, local_step(): swap = lambda x: lax.ppermute(x, 'sp', [(i, i ^ 1) for i in range(sp_size)])  36.3 us
  transfers between devices with their start and end apart: 9, of which 5 were waited for; matrix products, arithmetic and copies ran while one was open for 12% of the time, Pallas kernels for 45%

profile of v3, /device:TPU:0, one launch (start us, length us, event | category | flops | bytes accessed | tf_op | source)
XLA Modules:
  0.0 1033.6 jit_solution(640799467783546628)
XLA Ops:
  16.1 6.5 fusion.6.h_ref
  22.6 161.8 %gather_qkv.1 = (bf16[4096,4096]{1,0:T(8,128)(2,1)}, bf16[4096,4096]{1,0:T(8,128)(2,1)}, bf16[4096,512]{1,0:T(8,128)(2,1)}, bf16[4096,128]{1,0:T(8,128)(2,1)}, b...) custom-call(bf16[512,4096]{1,0:T(8,128)(2,1)} %fusion.6.h_ref, ...), custom_call_target="tpu_custom_call" | custom-call | tf_op jit(solution)/shard_map/gather_qkv/pallas_call | solution.py:174
  184.5 80.2 %attn_fwd.1 = (bf16[512,4096]{1,0:T(8,128)(2,1)}, f32[4,4096,1]{2,1,0:T(8,128)}) custom-call(bf16[4096,512]{1,0:T(8,128)(2,1)} %get-tuple-element.46.q_ref.refs_0_, bf16[128,4096]{1,0:T(8,128)(2,1)} %get-tuple-element.47.kt_ref.refs_4_, bf16[4096,128]{1,0:T(8,128)(2,1)} %get-tuple-element.48.v_ref), custom_call_target="tpu_custom_call" | custom-call | flops 68719476736 | bytes 16777216 | tf_op jit(solution)/shard_map/attn_fwd/pallas_call | solution.py:257
  264.7 75.1 %all-gather.10.cloned.1.call-done.g_ref = bf16[4096,4096]{1,0:T(8,128)(2,1)} async-done(((bf16[512,4096]{1,0:T(8,128)(2,1)}), bf16[4096,4096]{1,0:T(8,128)(2,1)}) %all-gather.10.cloned.1.call-update) | async-done | bytes 33554448 | tf_op jit(solution)/shard_map/all_gather | solution.py:449
  339.8 23.3 %do_proj.1.refs_1_ = bf16[4096,512]{1,0:T(8,128)(2,1)} custom-call(s32[1]{0:T(128)} %bitcast.1.dev_ref, bf16[4096,4096]{1,0:T(8,128)(2,1)} %all-gather.10.cloned.1.call-done.g_ref, bf16[4096,4096]{1,0:T(8,128)(2,1)} %wo_ref.1), custom_call_target="tpu_custom_call" | custom-call | flops 17179869184 | bytes 33554432 | tf_op jit(solution)/shard_map/do_proj/pallas_call | solution.py:193
  363.1 84.3 %attn_bwd.2 = (bf16[4096,256]{1,0:T(8,128)(2,1)}, f32[128,4096]{1,0:T(8,128)}, f32[128,4096]{1,0:T(8,128)}) custom-call(bf16[4096,512]{1,0:T(8,128)(2,1)} %get-tuple-element.46.q_ref.refs_0_, bf16[4096,512]{1,0:T(8,128)(2,1)} %do_proj.1.refs_1_, f32[4,4096,1]{2,1,0:T(8,128)} %get-tuple-element.53.refs_2_, bf16[4096,128]{1,0:T(8,128)(2,1)} %get-tuple-element.54.refs_3_, ...), custom_call_target="tpu_custom_call" | custom-call | flops 34359738368 | bytes 8388608 | tf_op jit(solution)/shard_map/attn_bwd/pallas_call | solution.py:334
  447.4 50.0 %all-gather.12.cloned.1.call-done = bf16[4096,4096]{1,0:T(8,128)(2,1)} async-done(((bf16[512,4096]{1,0:T(8,128)(2,1)}), bf16[4096,4096]{1,0:T(8,128)(2,1)}) %all-gather.12.cloned.1.call-update) | async-done | bytes 33554448 | tf_op jit(solution)/shard_map/all_gather | solution.py:452
  497.5 86.1 %attn_bwd.3 = (bf16[4096,256]{1,0:T(8,128)(2,1)}, f32[128,4096]{1,0:T(8,128)}, f32[128,4096]{1,0:T(8,128)}) custom-call(bf16[4096,512]{1,0:T(8,128)(2,1)} %get-tuple-element.46.q_ref.refs_0_, bf16[4096,512]{1,0:T(8,128)(2,1)} %do_proj.1.refs_1_, f32[4,4096,1]{2,1,0:T(8,128)} %get-tuple-element.53.refs_2_, bf16[4096,128]{1,0:T(8,128)(2,1)} %get-tuple-element.54.refs_3_, ...), custom_call_target="tpu_custom_call" | custom-call | flops 34359738368 | bytes 8388608 | tf_op jit(solution)/shard_map/attn_bwd/pallas_call | solution.py:334
  583.5 7.8 kv_grad.1
  591.4 81.2 %dw_o_half.1 = (bf16[4096,4096]{1,0:T(8,128)(2,1)}, bf16[2048,4096]{1,0:T(8,128)(2,1)}) custom-call(s32[1]{0:T(128)} %bitcast.13.core_ref, bf16[8,512,4096]{2,1,0:T(8,128)(2,1)} %bitcast.32, bf16[4096,4096]{1,0:T(8,128)(2,1)} %all-gather.10.cloned.1.call-done.g_ref), custom_call_target="tpu_custom_call" | custom-call | flops 68719476736 | bytes 100663296 | tf_op jit(solution)/shard_map/dw_o_half/pallas_call | solution.py:362
  676.7 22.1 %collective-permute-done.refs_0_ = bf16[2048,4096]{1,0:T(8,128)(2,1)} collective-permute-done((bf16[2048,4096]{1,0:T(8,128)(2,1)}, bf16[2048,4096]{1,0:T(8,128)(2,1)}, u32[]{:S(2)}, u32[]{:S(2)}) %collective-permute-start) | collective-permute-done | bytes 16777248 | tf_op jit(solution)/shard_map/ppermute | solution.py:464
  698.8 54.6 %dw_qa.1 = (bf16[4096,4096]{1,0:T(8,128)(2,1)}, bf16[4096,1024]{1,0:T(8,128)(2,1)}, bf16[4096,4096]{1,0:T(8,128)(2,1)}) custom-call(s32[1]{0:T(128)} %bitcast.13.core_ref, bf16[4096,4096]{1,0:T(8,128)(2,1)} %get-tuple-element.71.ht_ref, bf16[8,4096,256]{2,1,0:T(8,128)(2,1)} %bitcast.34, ...), custom_call_target="tpu_custom_call", output_to_operand_aliasing={{2}: (4, {})} | custom-call | flops 34359738368 | bytes 100663296 | tf_op jit(solution)/shard_map/dw_qa/pallas_call | solution.py:410
  753.6 14.3 %collective-permute-done.1.refs_0_ = bf16[4096,1024]{1,0:T(8,128)(2,1)} collective-permute-done((bf16[4096,1024]{1,0:T(8,128)(2,1)}, bf16[4096,1024]{1,0:T(8,128)(2,1)}, u32[]{:S(2)}, u32[]{:S(2)}) %collective-permute-start.1) | collective-permute-done | bytes 8388640 | tf_op jit(solution)/shard_map/ppermute | solution.py:464
  767.9 51.7 %dw_kv.1 = (bf16[4096,1024]{1,0:T(8,128)(2,1)}, bf16[4096,1024]{1,0:T(8,128)(2,1)}, bf16[4096,1024]{1,0:T(8,128)(2,1)}, bf16[4096,4096]{1,0:T(8,128)(2,1)}) custom-call(s32[1]{0:T(128)} %bitcast.13.core_ref, bf16[4096,4096]{1,0:T(8,128)(2,1)} %get-tuple-element.71.ht_ref, bf16[8,4096,256]{2,1,0:T(8,128)(2,1)} %bitcast.38, ...), custom_call_target="tpu_custom_call", output_to_operand_aliasing={{3}: (4, {})} | custom-call | flops 34359738368 | bytes 100663296 | tf_op jit(solution)/shard_map/dw_kv/pallas_call | solution.py:410
  822.5 23.1 %convolution_convert_fusion = bf16[512,4096]{1,0:T(8,128)(2,1)} fusion(bf16[4096,512]{1,0:T(8,128)(2,1)S(1)} %bitcast.28, bf16[4096,4096]{1,0:T(8,128)(2,1)} %wo_ref.1), kind=kOutput, calls=%fused_computation.15 | convolution fusion | flops 17181966336 | bytes 41943040 | tf_op jit(solution)/shard_map/et,ed->td/dot_general | solution.py:475
  858.4 5.8 copy.24
  864.2 52.1 %dw_qb.1 = (bf16[4096,4096]{1,0:T(8,128)(2,1)}, bf16[4096,1024]{1,0:T(8,128)(2,1)}, bf16[4096,1024]{1,0:T(8,128)(2,1)}, bf16[4096,1024]{1,0:T(8,128)(2,1)}) custom-call(s32[1]{0:T(128)} %bitcast.13.core_ref, bf16[4096,4096]{1,0:T(8,128)(2,1)} %get-tuple-element.71.ht_ref, ...), custom_call_target="tpu_custom_call", output_to_operand_aliasing={{0}: (5, {}), {2}: (6, {}), {3}: (7, {})} | custom-call | flops 34359738368 | bytes 100663296 | tf_op jit(solution)/shard_map/dw_qb/pallas_call | solution.py:410
  916.5 11.5 %fusion.14 = f32[512,4096]{1,0:T(8,128)} fusion(bf16[512,1024]{0,1:T(8,128)(2,1)} %bitcast.30, bf16[4096,1024]{1,0:T(8,128)(2,1)} %wk_ref.1), kind=kOutput, calls=%fused_computation.31 | convolution fusion | flops 4294967296 | bytes 17825792 | tf_op jit(solution)/shard_map/te,de->td/dot_general | solution.py:499
  936.9 6.5 copy.21
  943.4 24.5 %fusion.13 = f32[512,4096]{1,0:T(8,128)} fusion(bf16[512,4096]{0,1:T(8,128)(2,1)} %bitcast.29, bf16[4096,4096]{1,0:T(8,128)(2,1)} %wq_ref.1), kind=kOutput, calls=%fused_computation.30 | convolution fusion | flops 17179869184 | bytes 46137344 | tf_op jit(solution)/shard_map/te,de->td/dot_general | solution.py:498
  967.9 15.5 %fusion.7 = (f32[4096]{0:T(1024)S(1)}, f32[512]{0:T(512)S(1)}, f32[512,4096]{1,0:T(8,128)}) fusion(bf16[512,4096]{1,0:T(8,128)(2,1)S(1)} %copy-done, f32[512]{0:T(512)S(1)} %copy-done.9, f32[512]{0:T(512)S(1)} %copy-done.5, f32[4096]{0:T(1024)S(1)} %copy-done.3, bf16[512,1024]{0,1:T(8,128)(2,1)S(1)} %bitcast.31, bf16[4096,1024]{1,0:T(8,128)(2,1)} %wv_ref.1, ...), kind=kOutput, calls=%fused_computation.10 | convolution fusion | flops 4315934208 | bytes 38836224 | tf_op jit(solution)/shard_map/te,de->td/dot_general | solution.py:500
  983.4 22.3 %psum.7 = bf16[4096]{0:T(1024)(128)(2,1)} all-reduce(f32[4096]{0:T(1024)S(1)} %get-tuple-element.85), channel_id=1, replica_groups=mesh['dp'=1,'sp'=8] {'sp'}, use_global_device_ids=true, to_apply=%region_5.0 | all-reduce | flops 4096 | bytes 24576 | tf_op jit(solution)/shard_map/psum | solution.py:502
  1005.7 5.9 fusion.11
  1014.9 11.9 %copy_in.1 = bf16[4096,4096]{1,0:T(8,128)(2,1)} custom-call(s32[1]{0:T(128)} %bitcast.13.core_ref, bf16[4096,1024]{1,0:T(8,128)(2,1)} %collective-permute-done.3.recv_ref, bf16[4096,4096]{1,0:T(8,128)(2,1)} %get-tuple-element.81._), custom_call_target="tpu_custom_call", output_to_operand_aliasing={{}: (2, {})} | custom-call | tf_op jit(solution)/shard_map/copy_in/pallas_call | solution.py:424
  (61 shorter events, 41.5 us)
Async XLA Ops:
  7.2 8.2 copy-start.10
  7.2 332.6 %all-gather.10.cloned.1.call-start = ((), (), s32[]{:S(2)}) async-start(), calls=%async_computation | async-start | bytes 37748736 | tf_op jit(solution)/shard_map/all_gather | solution.py:449
  11.3 4.8 copy-start.4
  14.7 0.6 copy-start.6
  15.3 0.7 copy-start.8
  15.3 0.7 copy-start.2
  184.4 313.0 %all-gather.12.cloned.1.call-start = ((), (), s32[]{:S(2)}) async-start(), calls=%async_computation.1 | async-start | bytes 37748736 | tf_op jit(solution)/shard_map/all_gather | solution.py:452
  339.8 251.5 %all-gather.14.cloned.1.call-start = ((), (), s32[]{:S(2)}) async-start(), calls=%async_computation.2 | async-start | bytes 18874368 | tf_op jit(solution)/shard_map/all_gather | solution.py:456
  497.4 179.3 %all-gather.16.cloned.1.call-start = ((), (), s32[]{:S(2)}) async-start(), calls=%async_computation.3 | async-start | bytes 18874368 | tf_op jit(solution)/shard_map/all_gather | solution.py:460
  591.3 272.9 %all-gather.18.cloned.1.call-start = ((), (), s32[]{:S(2)}) async-start(), calls=%async_computation.4 | async-start | bytes 18874368 | tf_op jit(solution)/shard_map/all_gather | solution.py:462
  672.6 26.2 %collective-permute-start = (bf16[2048,4096]{1,0:T(8,128)(2,1)}, bf16[2048,4096]{1,0:T(8,128)(2,1)}, u32[]{:S(2)}, u32[]{:S(2)}) collective-permute-start(bf16[2048,4096]{1,0:T(8,128)(2,1)} %get-tuple-element.72), channel_id=1, source_target_pairs={{0,1},{1,0},{2,3},{3,2},{4,5},{5,4},{6,7},{7,6}} | collective-permute-start | bytes 50331656 | tf_op jit(solution)/shard_map/ppermute | solution.py:464
  753.3 14.6 %collective-permute-start.1 = (bf16[4096,1024]{1,0:T(8,128)(2,1)}, bf16[4096,1024]{1,0:T(8,128)(2,1)}, u32[]{:S(2)}, u32[]{:S(2)}) collective-permute-start(bf16[4096,1024]{1,0:T(8,128)(2,1)} %get-tuple-element.74), channel_id=1, source_target_pairs={{0,1},{1,0},{2,3},{3,2},{4,5},{5,4},{6,7},{7,6}} | collective-permute-start | bytes 25165832 | tf_op jit(solution)/shard_map/ppermute | solution.py:464
  819.7 44.5 %collective-permute-start.2 = (bf16[4096,1024]{1,0:T(8,128)(2,1)}, bf16[4096,1024]{1,0:T(8,128)(2,1)}, u32[]{:S(2)}, u32[]{:S(2)}) collective-permute-start(bf16[4096,1024]{1,0:T(8,128)(2,1)} %get-tuple-element.76), channel_id=1, source_target_pairs={{0,1},{1,0},{2,3},{3,2},{4,5},{5,4},{6,7},{7,6}} | collective-permute-start | bytes 25165832 | tf_op jit(solution)/shard_map/ppermute | solution.py:464
  916.3 98.6 %collective-permute-start.3 = (bf16[4096,1024]{1,0:T(8,128)(2,1)}, bf16[4096,1024]{1,0:T(8,128)(2,1)}, u32[]{:S(2)}, u32[]{:S(2)}) collective-permute-start(bf16[4096,1024]{1,0:T(8,128)(2,1)} %get-tuple-element.80), channel_id=1, source_target_pairs={{0,1},{1,0},{2,3},{3,2},{4,5},{5,4},{6,7},{7,6}} | collective-permute-start | bytes 25165832 | tf_op jit(solution)/shard_map/ppermute | solution.py:464
  928.0 6.5 copy-start.1
  943.3 24.5 %copy-start = (bf16[512,4096]{1,0:T(8,128)(2,1)S(1)}, bf16[512,4096]{1,0:T(8,128)(2,1)}, u32[]{:S(2)}) copy-start(bf16[512,4096]{1,0:T(8,128)(2,1)} %param.8) | copy-start | bytes 12582916
  943.3 24.5 %copy-start.3 = (f32[4096]{0:T(1024)S(1)}, f32[4096]{0:T(1024)}, u32[]{:S(2)}) copy-start(f32[4096]{0:T(1024)} %copy-done.2) | copy-start | bytes 49156
  943.3 24.5 %copy-start.5 = (f32[512]{0:T(512)S(1)}, f32[512]{0:T(512)}, u32[]{:S(2)}) copy-start(f32[512]{0:T(512)} %copy-done.4) | copy-start | bytes 6148
  943.3 24.5 %copy-start.9 = (f32[512]{0:T(512)S(1)}, f32[512]{0:T(512)}, u32[]{:S(2)}) copy-start(f32[512]{0:T(512)} %copy-done.8) | copy-start | bytes 6148
  967.9 37.8 %copy-start.7 = (f32[512]{0:T(512)S(1)}, f32[512]{0:T(512)}, u32[]{:S(2)}) copy-start(f32[512]{0:T(512)} %copy-done.6) | copy-start | bytes 6148
Sparse Core Ops, SparseCore 0:
  184.5 155.1 all-gather.9
  342.1 155.2 all-gather.11
  499.8 84.0 all-gather.13
  591.4 85.1 all-gather.15
  678.9 85.1 all-gather.17
